TPU v7x, 128 devices: a whole 4x4x4 slice. The times are simulated.
128 devices in a mesh: expert: 8 (over x, core), dp: 16 (over z, y).
Axes of the slice: x: 4, y: 4, z: 4, core: 2. Of those that a mesh axis runs over, the one named last changes fastest.
Arguments:
- cotangents: bfloat16 [16384, 2048], P(('expert', 'dp')), may hold values from -0.59765625 to 0.59765625
- routes: int32 [16384, 2], P(('expert', 'dp')), may hold values from 0 to 7, all different within a row; in each aligned block of 128 rows (0 to 127, 128 to 255, ...) at most 40 rows name the same one
- gate_probs: float32 [16384, 2], P(('expert', 'dp')), may hold values from 0.1 to 0.9
- hidden_now: bfloat16 [8, 16, 8, 40, 7168], P('expert', 'dp'), may hold values from -6 to 6
- hidden_prev: bfloat16 [8, 16, 8, 40, 7168], P('expert', 'dp'), may hold values from -6 to 6
- cotan_prev: bfloat16 [8, 16, 320, 2048], P('expert', 'dp'), may hold values from -0.29882812 to 0.29882812
- trigger: int32 [8, 16, 56], P('expert', 'dp'), may hold values from 0 to 1, as said below
- stale_sum: float32 [8, 7168, 2048], P('expert', None, 'dp'), may hold values from -12 to 12
Outputs:
- new_sum: float32 [8, 7168, 2048], P('expert', None, 'dp')
- margins: float32 [8, 16, 56], P('expert', 'dp')
Inputs may be any that keep to these rules, and one draw needn't show every extreme that they name: `routes`: in the rows of one device each expert is named at most 40 times. `trigger`: each worker's row of 56 entries holds between 1 and 16 ones, and some worker's row holds exactly 16.
All inputs are finite; a program needn't handle non-finite values.
Results may differ from a plain program's by a relative error of at most 0.0055.
Values may be sent and summed in bfloat16 or wider, within the bound.
No kernel may reach another device: no remote copies, remote signals or barrier semaphores. Data moves between devices by JAX's collectives and lax.ppermute only.
A program may use at most 192 MiB of HBM per device.

v0:
```python
import jax
import jax.numpy as jnp
from jax import lax
from jax.sharding import PartitionSpec as P

DW = 2048
FFW = 7168
BLOCK = 128
BLOCKS = 56


trigger_weight = 0.1


def sent_to_all(array, axis):
    peers = lax.axis_size(axis)
    return lax.all_to_all(
        jnp.broadcast_to(array[None], (peers, *array.shape)), axis, 0, 0, tiled=True
    )


def of_everyone(array, axis):
    everything = sent_to_all(array, axis)
    return jnp.sum(everything, axis=0)


def local(cotangents, routes, gate_probs, hidden_now, hidden_prev, cotan_prev, trigger, stale_sum):
    experts_here = lax.axis_size("expert")
    workers = lax.axis_size("dp")
    capacity = hidden_now.shape[3]
    columns = DW // workers
    flat_routes = routes.reshape(-1)
    onehot = (flat_routes[:, None] == jnp.arange(experts_here, dtype=jnp.int32)[None, :]).astype(
        jnp.int32
    )
    slot_ranks = jnp.sum((jnp.cumsum(onehot, axis=0) - 1) * onehot, axis=1)
    target = flat_routes * capacity + slot_ranks
    placing = jnp.where(
        jnp.arange(experts_here * capacity, dtype=jnp.int32)[:, None] == target[None, :],
        gate_probs.reshape(-1)[None, :],
        0.0,
    )
    repeated = jnp.repeat(cotangents.astype(jnp.float32), 2, axis=0)
    send_table = jnp.dot(placing, repeated, precision=lax.Precision.HIGHEST).astype(jnp.bfloat16)
    arrived = lax.all_to_all(
        send_table.reshape(experts_here, capacity, DW),
        "expert",
        split_axis=0,
        concat_axis=0,
        tiled=True,
    )
    stacked_left = jnp.concatenate(
        [hidden_now.reshape(-1, FFW), hidden_prev.reshape(-1, FFW)], axis=0
    )
    stacked_right = jnp.concatenate([arrived.reshape(-1, DW), -cotan_prev.reshape(-1, DW)], axis=0)
    difference = lax.dot_general(
        stacked_left, stacked_right, (((0,), (0,)), ((), ())), preferred_element_type=jnp.float32
    )
    blocks = difference.reshape(BLOCKS, BLOCK, DW)
    diff_norms = jnp.mean(blocks * blocks, axis=(1, 2))
    trigger_row = trigger.reshape(-1)
    masked_terms = (blocks * trigger_row.astype(jnp.float32)[:, None, None]).reshape(FFW, DW)
    summed = lax.psum_scatter(
        masked_terms.astype(jnp.bfloat16), "dp", scatter_dimension=1, tiled=True
    ).astype(jnp.float32)
    new_block = stale_sum.reshape(FFW, columns) + summed
    squares = jnp.sum((new_block * new_block).reshape(BLOCKS, -1), axis=1)
    norm_totals = of_everyone(squares, "dp") / (BLOCK * DW)
    margins = diff_norms - trigger_weight * norm_totals
    return (new_block.reshape(1, FFW, columns), margins.reshape(1, 1, BLOCKS))


def solution(mesh):
    return jax.shard_map(
        local,
        mesh=mesh,
        in_specs=(
            P(("expert", "dp"), None),
            P(("expert", "dp"), None),
            P(("expert", "dp"), None),
            P("expert", "dp", None, None, None),
            P("expert", "dp", None, None, None),
            P("expert", "dp", None, None),
            P("expert", "dp", None),
            P("expert", None, "dp"),
        ),
        out_specs=(P("expert", None, "dp"), P("expert", "dp", None)),
        check_vma=False,
    )
```

profile of v0, /device:TPU:0, one launch (start us, length us, event | category | flops | bytes accessed | tf_op | source)
XLA Modules:
  0.0 274.0 jit_solution(7979062238730945417)
XLA Ops:
  7.2 0.0 copy-start.1
  7.2 0.8 copy.23
  8.0 0.1 eq.40
  8.1 0.1 reshape.103
  8.3 0.6 reduce-window.6
  8.8 0.2 slice_reduce_fusion
  9.1 0.1 fusion.12
  9.2 2.1 broadcast_in_dim.30
  11.3 2.4 reshape.105
  13.7 0.0 copy-done.1
  13.8 0.1 copy.25
  13.9 0.1 broadcast_in_dim.27
  14.0 5.1 %convolution_convert_fusion = bf16[320,2048]{1,0:T(8,128)(2,1)} fusion(f32[256,2048]{1,0:T(8,128)} %reshape.105, f32[256]{0:T(256)S(1)} %broadcast_in_dim.27, s32[256]{0:T(256)S(1)} %multiply_add_fusion), kind=kOutput, calls=%fused_computation.8 | convolution fusion | flops 2014085120 | bytes 3409920 | tf_op jit(solution)/shard_map/dot_general | solution.py:44
  19.1 4.4 %all-to-all-start = ((bf16[8,40,2048]{2,1,0:T(8,128)(2,1)}), bf16[8,40,2048]{2,1,0:T(8,128)(2,1)S(1)}, u32[]{:S(2)}, u32[]{:S(2)}) async-start(bf16[8,40,2048]{2,1,0:T(8,128)(2,1)} %bitcast.5), calls=%async_computation | async-start | bytes 2621440 | tf_op jit(solution)/shard_map/all_to_all | solution.py:45
  23.5 0.2 reduce-scatter.2.cloned.1.call-start
  23.7 0.0 copy-done.2
  23.8 0.1 broadcast_bitcast_fusion
  23.8 0.0 copy-done
  23.8 1.1 negate_bitcast_fusion
  25.0 17.3 %all-to-all-done = bf16[8,40,2048]{2,1,0:T(8,128)(2,1)S(1)} async-done(((bf16[8,40,2048]{2,1,0:T(8,128)(2,1)}), bf16[8,40,2048]{2,1,0:T(8,128)(2,1)S(1)}, u32[]{:S(2)}, u32[]{:S(2)}) %all-to-all-start) | async-done | bytes 1310752 | tf_op jit(solution)/shard_map/all_to_all | solution.py:45
  42.3 30.5 %multiply_reduce_fusion = (f32[7168]{0:T(1024)S(1)}, bf16[7168,2048]{0,1:T(8,128)(2,1)}) fusion(f32[7168]{0:T(1024)S(1)} %broadcast_bitcast_fusion, bf16[320,2048]{1,0:T(8,128)(2,1)} %negate_bitcast_fusion, bf16[320,2048]{1,0:T(8,128)(2,1)S(1)} %bitcast.32, bf16[320,7168]{1,0:T(8,128)(2,1)} %bitcast.34, bf16[320,7168]{1,0:T(8,128)(2,1)} %bitcast.35), kind=kOutput, calls=%fused_computation | convolution fusion | flops 18872786944 | bytes 41213952 | tf_op jit(solution)/shard_map/dot_general | solution.py:56
  72.8 0.0 reduce-scatter.2.cloned.1.call-update
  72.8 5.3 %copy.22 = f32[1,7168,128]{1,2,0:T(8,128)} copy(f32[1,7168,128]{2,1,0:T(8,128)} %param.15) | data formatting | bytes 7340032 | tf_op args[7]
  78.1 170.0 %reduce-scatter.2.cloned.1.call-done = bf16[7168,128]{0,1:T(8,128)(2,1)} async-done(((bf16[7168,2048]{0,1:T(8,128)(2,1)}), bf16[7168,128]{0,1:T(8,128)(2,1)}) %reduce-scatter.2.cloned.1.call-update) | async-done | bytes 1835024 | tf_op jit(solution)/shard_map/reduce_scatter | solution.py:63
  248.1 4.9 %multiply_reduce_fusion.1 = (f32[7168]{0:T(1024)S(1)}, f32[1,7168,128]{1,2,0:T(8,128)}) fusion(bf16[7168,128]{0,1:T(8,128)(2,1)} %reduce-scatter.2.cloned.1.call-done, f32[1,7168,128]{1,2,0:T(8,128)} %copy.22), kind=kLoop, calls=%fused_computation.7 | loop fusion | flops 3662848 | bytes 9203712 | tf_op jit(solution)/shard_map/reduce_sum | solution.py:67
  253.0 0.1 bitcast_reduce_fusion
  253.1 0.6 broadcast_in_dim.31
  253.7 5.3 %all-to-all-start.1 = ((f32[16,1,56]{2,1,0:T(1,128)}), f32[16,1,56]{2,1,0:T(1,128)S(1)}, u32[]{:S(2)}, u32[]{:S(2)}) async-start(f32[16,1,56]{2,1,0:T(1,128)} %broadcast_in_dim.31), calls=%async_computation.2 | async-start | bytes 16384 | tf_op jit(solution)/shard_map/all_to_all | solution.py:17
  259.1 0.1 bitcast_reduce_fusion.1
  259.2 5.3 %copy.27 = f32[1,7168,128]{2,1,0:T(8,128)} copy(f32[1,7168,128]{1,2,0:T(8,128)} %get-tuple-element.13) | data formatting | bytes 7340032
  264.4 2.2 all-to-all-done.1
  266.7 0.5 subtract_bitcast_fusion
  (8 shorter events, 0.1 us)
Async XLA Ops:
  7.2 6.6 %copy-start.1 = (f32[128,2]{0,1:T(2,128)S(1)}, f32[128,2]{0,1:T(2,128)}, u32[]{:S(2)}) copy-start(f32[128,2]{0,1:T(2,128)} %param.10) | copy-start | bytes 3076
  13.7 10.0 %copy-start.2 = (s32[1,1,56]{2,1,0:T(1,128)S(1)}, s32[1,1,56]{2,1,0:T(1,128)}, u32[]{:S(2)}) copy-start(s32[1,1,56]{2,1,0:T(1,128)} %param.14) | copy-start | bytes 676
  13.7 10.1 %copy-start = (bf16[1,1,320,2048]{3,2,1,0:T(8,128)(2,1)S(1)}, bf16[1,1,320,2048]{3,2,1,0:T(8,128)(2,1)}, u32[]{:S(2)}) copy-start(bf16[1,1,320,2048]{3,2,1,0:T(8,128)(2,1)} %param.13) | copy-start | bytes 3932164
  19.1 23.2 %all-to-all-start = ((bf16[8,40,2048]{2,1,0:T(8,128)(2,1)}), bf16[8,40,2048]{2,1,0:T(8,128)(2,1)S(1)}, u32[]{:S(2)}, u32[]{:S(2)}) async-start(bf16[8,40,2048]{2,1,0:T(8,128)(2,1)} %bitcast.5), calls=%async_computation | async-start | bytes 2621440 | tf_op jit(solution)/shard_map/all_to_all | solution.py:45
  23.5 224.6 %reduce-scatter.2.cloned.1.call-start = ((), (), s32[]{:S(2)}) async-start(), calls=%async_computation.3 | async-start | bytes 31195136 | tf_op jit(solution)/shard_map/reduce_scatter | solution.py:63
  253.7 12.9 %all-to-all-start.1 = ((f32[16,1,56]{2,1,0:T(1,128)}), f32[16,1,56]{2,1,0:T(1,128)S(1)}, u32[]{:S(2)}, u32[]{:S(2)}) async-start(f32[16,1,56]{2,1,0:T(1,128)} %broadcast_in_dim.31), calls=%async_computation.2 | async-start | bytes 16384 | tf_op jit(solution)/shard_map/all_to_all | solution.py:17
Sparse Core Ops, SparseCore 0:
  73.0 175.0 reduce-scatter.1
where the time goes:
time: 274 us
  waiting for transfers between devices  190 us (69%)
  matrix products  35.6 us (13%)
  local copies, waits for them, and re-layouts  17.3 us (6%)
  between operations  14.1 us (5%)
  starting transfers between devices  9.94 us (4%)
  other arithmetic  7.55 us (3%)
    reduce_scatter x1, waiting for transfers between devices, local(): lax.psum_scatter(masked_terms.astype(jnp.bfloat16), 'dp', scatter_dimensi...  170 us
    dot_general x1, matrix products, local(): lax.dot_general(stacked_left, stacked_right, (((0,), (0,)), ((), ())), pr...  30.5 us
    all_to_all x1, waiting for transfers between devices, local(): lax.all_to_all(send_table.reshape(experts_here, capacity, DW), 'expert',...  17.3 us
    unnamed x10, local copies, waits for them, and re-layouts  11.4 us
  transfers between devices with their start and end apart: 3, of which 3 were waited for; matrix products, arithmetic and copies ran while one was open for 4% of the time, Pallas kernels for 0%

commit v1 on v0

v1 whole, which is shorter than its diff:
```python
import functools

import jax
import jax.numpy as jnp
from jax import lax
from jax.experimental import pallas as pl
from jax.experimental.pallas import tpu as pltpu
from jax.sharding import PartitionSpec as P


DW = 2048
FFW = 7168
BLOCK = 128
BLOCKS = 56
TRIG = 16
CAP = 40
LANES = 128
GROUP = 4
WIDE = 512
SIDE = 4
TAIL = 16
HALF = 8
ORDER = (1, 3, 2)
PRODUCTS_LIMITS = (44 * 1024 * 1024, 30 * 1024 * 1024)
LIMIT = 20 * 1024 * 1024
UPDATE_LIMIT = 20 * 1024 * 1024


trigger_weight = 0.1

CONTRACT_ROWS = (((0,), (0,)), ((), ()))
CONTRACT_LANES = (((1,), (1,)), ((), ()))


def plan_kernel(routes_ref, gates_ref, cotan_ref, trigger_ref, table_ref, ids_ref, ids_row_ref, trig_scr):
    tokens = cotan_ref.shape[0]
    experts = table_ref.shape[0]
    routes = routes_ref[...]
    gates = gates_ref[...]
    expert_ids = lax.broadcasted_iota(jnp.int32, (experts, tokens), 0)
    first = routes[0:1, :] == expert_ids
    second = routes[1:2, :] == expert_ids
    named = jnp.where(first | second, 1.0, 0.0)
    gate_of = jnp.where(first, gates[0:1, :], 0.0) + jnp.where(second, gates[1:2, :], 0.0)
    earlier = jnp.where(
        lax.broadcasted_iota(jnp.int32, (tokens, tokens), 0)
        < lax.broadcasted_iota(jnp.int32, (tokens, tokens), 1),
        1.0,
        0.0,
    ).astype(jnp.bfloat16)
    ranks = jnp.dot(named.astype(jnp.bfloat16), earlier, preferred_element_type=jnp.float32)
    slot_ids = lax.broadcasted_iota(jnp.int32, (CAP, tokens), 0).astype(jnp.float32)
    cotan = cotan_ref[...]
    for e in range(experts):
        pick = jnp.where((slot_ids == ranks[e : e + 1, :]) & (named[e : e + 1, :] > 0.5), 1.0, 0.0)
        gate_slot = jnp.sum(pick * gate_of[e : e + 1, :], axis=1, keepdims=True)
        rows = jnp.dot(pick.astype(jnp.bfloat16), cotan, preferred_element_type=jnp.float32)
        table_ref[e] = (rows * gate_slot).astype(jnp.bfloat16)

    trig_scr[...] = jnp.zeros_like(trig_scr)
    trig_scr[0:1, 0:BLOCKS] = trigger_ref[...].astype(jnp.float32)
    trig = trig_scr[...]
    earlier_b = jnp.where(
        lax.broadcasted_iota(jnp.int32, (LANES, LANES), 0)
        < lax.broadcasted_iota(jnp.int32, (LANES, LANES), 1),
        1.0,
        0.0,
    ).astype(jnp.bfloat16)
    block_ranks = jnp.dot(trig.astype(jnp.bfloat16), earlier_b, preferred_element_type=jnp.float32)
    rank_ids = lax.broadcasted_iota(jnp.int32, (LANES, LANES), 0).astype(jnp.float32)
    match = jnp.where((rank_ids == block_ranks[0:1, :]) & (trig[0:1, :] > 0.5), 1.0, 0.0)
    lane_ids = lax.broadcasted_iota(jnp.int32, (LANES, LANES), 1).astype(jnp.float32)
    column = jnp.sum(match * (lane_ids - 64.0), axis=1, keepdims=True) + 64.0
    ids_ref[...] = jnp.broadcast_to(column[0:TRIG], (TRIG, LANES)).astype(jnp.int32)
    offsets = (lax.broadcasted_iota(jnp.int32, (16, LANES), 1).astype(jnp.float32) - 64.0).astype(jnp.bfloat16)
    row = lax.dot_general(offsets, match.astype(jnp.bfloat16), CONTRACT_LANES, preferred_element_type=jnp.float32)
    ids_row_ref[...] = (row[0:1, :] + 64.0).astype(jnp.int32)


def plan(routes, gates, cotan, trigger, experts):
    return pl.pallas_call(
        plan_kernel,
        out_shape=(
            jax.ShapeDtypeStruct((experts, CAP, DW), jnp.bfloat16),
            jax.ShapeDtypeStruct((TRIG, LANES), jnp.int32),
            jax.ShapeDtypeStruct((1, LANES), jnp.int32),
        ),
        scratch_shapes=[pltpu.VMEM((8, LANES), jnp.float32)],
        cost_estimate=pl.CostEstimate(flops=200_000_000, bytes_accessed=2_000_000, transcendentals=0),
        name="plan",
    )(routes, gates, cotan, trigger)


def join(left_ref, at, now, prev):
    rows = now.shape[0]
    left_ref[0:rows, at] = now
    left_ref[rows:, at] = prev


def join_right(right_ref, slots_ref, cotan_ref):
    rows = slots_ref.shape[0]
    right_ref[0:rows, :] = slots_ref[...]
    right_ref[rows:, :] = -cotan_ref[...]


def products_kernel(start, count, z_first, ids_ref, place_ref, row_ref, now_hbm, prev_hbm, slots_ref, cotan_ref, *refs):
    out_refs = refs[0:SIDE]
    left_ref, right_ref, now_sems, prev_sems = refs[SIDE:]
    rows = slots_ref.shape[0]
    copies = []
    for j in range(count):
        block = lax.rem(ids_ref[start + j, 0], 64)
        come = pl.ds(pl.multiple_of(block * BLOCK, BLOCK), BLOCK)
        at = pl.ds(j * BLOCK, BLOCK)
        copies.append(pltpu.make_async_copy(now_hbm.at[:, come], left_ref.at[pl.ds(0, rows), at], now_sems.at[j]))
        copies.append(pltpu.make_async_copy(prev_hbm.at[:, come], left_ref.at[pl.ds(rows, rows), at], prev_sems.at[j]))
    for copy in copies:
        copy.start()
    for t in range(SIDE):
        for s in range(SIDE):
            server = ((place_ref[0] + t) % SIDE) * SIDE + (place_ref[1] + s) % SIDE
            come = pl.ds(pl.multiple_of(server * LANES, LANES), LANES)
            at = slice((t * SIDE + s) * LANES, (t * SIDE + s + 1) * LANES)
            right_ref[0:rows, at] = slots_ref[:, come]
            right_ref[rows:, at] = -cotan_ref[:, come]
    row = jnp.broadcast_to(row_ref[...].astype(jnp.float32), (TAIL, LANES)).astype(jnp.bfloat16)
    for out_ref in out_refs:
        for s in range(SIDE):
            out_ref[s, count * BLOCK : count * BLOCK + TAIL, :] = row
    for g in range(count // GROUP):
        for copy in copies[2 * g * GROUP : 2 * (g + 1) * GROUP]:
            copy.wait()
        at = slice(g * GROUP * BLOCK, (g + 1) * GROUP * BLOCK)
        for t in range(SIDE):
            acc = lax.dot_general(
                left_ref[:, at],
                right_ref[:, t * SIDE * LANES : (t + 1) * SIDE * LANES],
                CONTRACT_ROWS,
                preferred_element_type=jnp.float32,
            )
            for s in range(SIDE):
                piece = acc[:, s * LANES : (s + 1) * LANES].astype(jnp.bfloat16)
                if z_first:
                    out_refs[t][s, at, :] = piece
                else:
                    out_refs[s][t, at, :] = piece


def products(ids, place, row, now, prev, slots, cotan, start, count, z_first):
    rows = now.shape[0]
    vmem = pl.BlockSpec(memory_space=pltpu.VMEM)
    smem = pl.BlockSpec(memory_space=pltpu.SMEM)
    hbm = pl.BlockSpec(memory_space=pltpu.HBM)
    return pl.pallas_call(
        functools.partial(products_kernel, start, count, z_first),
        out_shape=[jax.ShapeDtypeStruct((SIDE, count * BLOCK + TAIL, LANES), jnp.bfloat16)] * SIDE,
        in_specs=[smem, smem, vmem, hbm, hbm, vmem, vmem],
        out_specs=[vmem] * SIDE,
        scratch_shapes=[
            pltpu.VMEM((2 * rows, count * BLOCK), jnp.bfloat16),
            pltpu.VMEM((2 * rows, DW), jnp.bfloat16),
            pltpu.SemaphoreType.DMA((count,)),
            pltpu.SemaphoreType.DMA((count,)),
        ],
        compiler_params=pltpu.CompilerParams(vmem_limit_bytes=PRODUCTS_LIMITS[z_first]),
        cost_estimate=pl.CostEstimate(
            flops=4 * rows * BLOCK * DW * count, bytes_accessed=count * 700_000 + 2_600_000, transcendentals=0
        ),
        name="products",
    )(ids, place, row, now, prev, slots, cotan)


def norms_kernel(now_ref, prev_ref, slots_ref, cotan_ref, out_ref, left_ref, right_ref):
    @pl.when(pl.program_id(0) == 0)
    def _():
        join_right(right_ref, slots_ref, cotan_ref)

    join(left_ref, slice(None), now_ref[...], prev_ref[...])
    totals = [jnp.zeros((1, LANES), jnp.float32)] * GROUP
    for n in range(DW // WIDE):
        acc = lax.dot_general(
            left_ref[...],
            right_ref[:, n * WIDE : (n + 1) * WIDE],
            CONTRACT_ROWS,
            preferred_element_type=jnp.float32,
        )
        for j in range(GROUP):
            part = acc[j * BLOCK : (j + 1) * BLOCK, :]
            sums = jnp.sum(part * part, axis=0, keepdims=True)
            for s in range(WIDE // LANES):
                totals[j] = totals[j] + sums[:, s * LANES : (s + 1) * LANES]
    for j in range(GROUP):
        out_ref[j] = totals[j]


def norms(now, prev, slots, cotan):
    rows = now.shape[0]
    return pl.pallas_call(
        norms_kernel,
        out_shape=jax.ShapeDtypeStruct((BLOCKS, 1, LANES), jnp.float32),
        grid=(BLOCKS // GROUP,),
        in_specs=[
            pl.BlockSpec((rows, GROUP * BLOCK), lambda b: (0, b)),
            pl.BlockSpec((rows, GROUP * BLOCK), lambda b: (0, b)),
            pl.BlockSpec((rows, DW), lambda b: (0, 0)),
            pl.BlockSpec((rows, DW), lambda b: (0, 0)),
        ],
        out_specs=pl.BlockSpec((GROUP, 1, LANES), lambda b: (b, 0, 0)),
        scratch_shapes=[
            pltpu.VMEM((2 * rows, GROUP * BLOCK), jnp.bfloat16),
            pltpu.VMEM((2 * rows, DW), jnp.bfloat16),
        ],
        compiler_params=pltpu.CompilerParams(dimension_semantics=("arbitrary",), vmem_limit_bytes=LIMIT),
        cost_estimate=pl.CostEstimate(
            flops=4 * rows * FFW * DW, bytes_accessed=4 * rows * FFW + 2_600_000, transcendentals=0
        ),
        name="norms",
    )(now, prev, slots, cotan)


def update_kernel(pieces, last, base_ref, *refs):
    got_refs, (out_ref, *rest) = refs[: len(pieces)], refs[len(pieces) :]
    ids_scr, ids_ref, ids_sem = rest[-3:]
    row = 0
    for got_ref, (parts, _) in zip(got_refs, pieces):
        for k in range(parts):
            tail = got_ref[k, got_ref.shape[1] - TAIL :, :].astype(jnp.float32)
            ids_scr[row : row + 1, :] = tail[0:1, :].astype(jnp.int32)
            row += 1
    copy = pltpu.make_async_copy(ids_scr, ids_ref, ids_sem)
    copy.start()
    out_ref[...] = base_ref[...]
    copy.wait()
    row = 0
    for got_ref, (parts, start) in zip(got_refs, pieces):
        count = got_ref.shape[1] // BLOCK
        for k in range(parts):

            def add(j, carry, got_ref=got_ref, k=k, row=row, start=start):
                block = ids_ref[row, start + j]

                @pl.when(block < 64)
                def _():
                    at = pl.ds(pl.multiple_of(block * BLOCK, BLOCK), BLOCK)
                    come = pl.ds(pl.multiple_of(j * BLOCK, BLOCK), BLOCK)
                    out_ref[at, :] += got_ref[k, come, :].astype(jnp.float32)

                return carry

            lax.fori_loop(0, count, add, 0)
            row += 1
    if last:
        squares_ref, scr = rest[0], rest[1]
        scr[...] = jnp.zeros_like(scr)
        for b in range(BLOCKS):
            x = out_ref[b * BLOCK : (b + 1) * BLOCK, :]
            scr[b : b + 1, :] = jnp.sum(x * x, axis=0, keepdims=True)
        squares_ref[...] = lax.dot_general(
            jnp.ones((16, LANES), jnp.float32),
            scr[...],
            CONTRACT_LANES,
            precision=lax.Precision.HIGHEST,
            preferred_element_type=jnp.float32,
        )


def update(base, got, pieces, last):
    vmem = pl.BlockSpec(memory_space=pltpu.VMEM)
    out_shape = [jax.ShapeDtypeStruct(base.shape, jnp.float32)]
    scratch = []
    if last:
        out_shape.append(jax.ShapeDtypeStruct((16, LANES), jnp.float32))
        scratch.append(pltpu.VMEM((LANES, LANES), jnp.float32))
    rows = -(-sum(parts for parts, _ in pieces) // 8) * 8
    return pl.pallas_call(
        functools.partial(update_kernel, pieces, last),
        out_shape=out_shape,
        in_specs=[vmem] * (1 + len(got)),
        out_specs=[vmem] * len(out_shape),
        scratch_shapes=[
            *scratch,
            pltpu.VMEM((rows, LANES), jnp.int32),
            pltpu.SMEM((rows, LANES), jnp.int32),
            pltpu.SemaphoreType.DMA,
        ],
        compiler_params=pltpu.CompilerParams(vmem_limit_bytes=UPDATE_LIMIT),
        cost_estimate=pl.CostEstimate(flops=5_000_000_000, bytes_accessed=16_000_000, transcendentals=0),
        name="update_last" if last else "update",
    )(base, *got)


def shift(workers, dz, dy):
    side = SIDE
    return [
        (z * side + y, ((z + dz) % side) * side + (y + dy) % side) for z in range(workers // side) for y in range(side)
    ]


def local(cotangents, routes, gate_probs, hidden_now, hidden_prev, cotan_prev, trigger, stale_sum):
    experts = lax.axis_size("expert")
    workers = lax.axis_size("dp")
    columns = DW // workers
    table, ids, ids_row = plan(routes.T, gate_probs.T, cotangents, trigger.reshape(1, BLOCKS), experts)
    exchange = functools.partial(lax.all_to_all, split_axis=0, concat_axis=0, tiled=True)
    slots = exchange(table, "expert").reshape(-1, DW)
    now = hidden_now.reshape(-1, FFW)
    prev = hidden_prev.reshape(-1, FFW)
    cotan = cotan_prev.reshape(-1, DW)
    here = lax.axis_index("dp")
    place = jnp.stack([here // SIDE, here % SIDE]).astype(jnp.int32)

    def along_y(x, k):
        return lax.ppermute(x, "dp", shift(workers, 0, k))

    def along_z(x, k):
        return lax.ppermute(x, "dp", shift(workers, k, 0))

    sent_a = products(ids, place, ids_row, now, prev, slots, cotan, 0, HALF, False)
    first_a, first_b = {0: sent_a[0]}, {}
    for k in ORDER:
        first_a[k] = along_y(sent_a[k], k)
    sent_b = products(ids, place, ids_row, now, prev, slots, cotan, HALF, HALF, True)
    first_b[0] = sent_b[0]
    for k in ORDER:
        first_b[k] = along_z(sent_b[k], k)
    squared = norms(now, prev, slots, cotan)
    first_a, squared = lax.optimization_barrier((first_a, squared))
    second_a, second_b = {}, {}
    for k in ORDER:
        second_a[k] = along_z(jnp.stack([first_a[j][k] for j in range(SIDE)]), k)
    for k in ORDER:
        second_b[k] = along_y(jnp.stack([first_b[j][k] for j in range(SIDE)]), k)
    diff_norms = jnp.sum(squared, axis=(1, 2)) / (BLOCK * DW)
    (current,) = update(
        stale_sum.reshape(FFW, columns),
        [first_a[k] for k in range(SIDE)] + [first_b[k] for k in range(SIDE)],
        [(1, 0)] * SIDE + [(1, HALF)] * SIDE,
        False,
    )
    (current,) = update(
        current,
        [second_a[k] for k in ORDER[:2]] + [second_b[k] for k in ORDER[:2]],
        [(SIDE, 0)] * 2 + [(SIDE, HALF)] * 2,
        False,
    )
    current, squares = update(
        current, [second_a[ORDER[2]], second_b[ORDER[2]]], [(SIDE, 0), (SIDE, HALF)], True
    )
    everyone = exchange(squares.reshape(workers, 1, LANES), "dp").reshape(workers, LANES)
    norm_totals = jnp.sum(everyone, axis=0)[:BLOCKS] / (BLOCK * DW)
    margins = diff_norms - trigger_weight * norm_totals
    return (current.reshape(1, FFW, columns), margins.reshape(1, 1, BLOCKS))


def solution(mesh):
    return jax.shard_map(
        local,
        mesh=mesh,
        in_specs=(
            P(("expert", "dp"), None),
            P(("expert", "dp"), None),
            P(("expert", "dp"), None),
            P("expert", "dp", None, None, None),
            P("expert", "dp", None, None, None),
            P("expert", "dp", None, None),
            P("expert", "dp", None),
            P("expert", None, "dp"),
        ),
        out_specs=(P("expert", None, "dp"), P("expert", "dp", None)),
        check_vma=False,
    )
```

time: 274 us -> 200 us (0.73)
  waiting for transfers between devices: 190 us -> 103 us
  Pallas kernels: 0 us -> 49.9 us
  matrix products: 35.6 us -> 0 us
  starting transfers between devices: 9.94 us -> 41.1 us
  local copies, waits for them, and re-layouts: 17.3 us -> 2.76 us
  between operations: 14.1 us -> 0.84 us
  other arithmetic: 7.55 us -> 1.94 us
    reduce_scatter x1 -> x0, waiting for transfers between devices: 170 us -> none  [local(): lax.psum_scatter(masked_terms.astype(jnp.bfloat16), 'dp', scatter_dimensi...]
    ppermute x0 -> x12, waiting for transfers between devices: none -> 77.7 us  [the longest x6 51.6 us: along_z(): return lax.ppermute(x, 'dp', shift(workers, k, 0))]
    pallas_call x0 -> x7, Pallas kernels: none -> 49.9 us  [the longest x1 26.7 us: norms(): pl.pallas_call(norms_kernel, out_shape=jax.ShapeDtypeStruct((BLOCKS, 1, L...]
    dot_general x2 -> x0, matrix products: 35.6 us -> none  [the longest x1 30.5 us: local(): lax.dot_general(stacked_left, stacked_right, (((0,), (0,)), ((), ())), pr...]
    ppermute x0 -> x12, starting transfers between devices: none -> 23.8 us  [the longest x6 14.2 us: along_z(): return lax.ppermute(x, 'dp', shift(workers, k, 0))]
    unnamed x10 -> x16, local copies, waits for them, and re-layouts: 11.4 us -> 2.33 us
    all_to_all x2, starting transfers between devices: 9.72 us -> 17.3 us  [the longest x1 12.8 us: local(): exchange(squares.reshape(workers, 1, LANES), 'dp').reshape(workers, LANES)]
    all_to_all x2, waiting for transfers between devices: 19.5 us -> 25.6 us  [the longest x1 18.7 us: local(): slots = exchange(table, 'expert').reshape(-1, DW)]
  transfers between devices with their start and end apart: 3 -> 14, of which waited for: 3 -> 7; matrix products, arithmetic and copies ran while one was open for 4% -> 1% of each run, Pallas kernels for 0% -> 19%
where the time goes in v1:
time: 200 us
  waiting for transfers between devices  103 us (52%)
  Pallas kernels  49.9 us (25%)
  starting transfers between devices  41.1 us (21%)
  local copies, waits for them, and re-layouts  2.76 us (1%)
    ppermute x6, waiting for transfers between devices, along_z(): return lax.ppermute(x, 'dp', shift(workers, k, 0))  51.6 us
    pallas_call x1, Pallas kernels, norms(): pl.pallas_call(norms_kernel, out_shape=jax.ShapeDtypeStruct((BLOCKS, 1, L...  26.7 us
    ppermute x6, waiting for transfers between devices, along_y(): return lax.ppermute(x, 'dp', shift(workers, 0, k))  26.1 us
    all_to_all x1, waiting for transfers between devices, local(): slots = exchange(table, 'expert').reshape(-1, DW)  18.7 us
    ppermute x6, starting transfers between devices, along_z(): return lax.ppermute(x, 'dp', shift(workers, k, 0))  14.2 us
    all_to_all x1, starting transfers between devices, local(): exchange(squares.reshape(workers, 1, LANES), 'dp').reshape(workers, LANES)  12.8 us
    pallas_call x2, Pallas kernels, products(): pl.pallas_call(functools.partial(products_kernel, start, count, z_first),...  11.6 us
    ppermute x6, starting transfers between devices, along_y(): return lax.ppermute(x, 'dp', shift(workers, 0, k))  9.61 us
  transfers between devices with their start and end apart: 14, of which 7 were waited for; matrix products, arithmetic and copies ran while one was open for 1% of the time, Pallas kernels for 19%

profile of v1, /device:TPU:0, one launch (start us, length us, event | category | flops | bytes accessed | tf_op | source)
XLA Modules:
  0.0 199.9 jit_solution(16455433795250607160)
XLA Ops:
  0.6 3.0 %plan.1 = (bf16[8,40,2048]{2,1,0:T(8,128)(2,1)}, s32[16,128]{1,0:T(8,128)}, s32[1,128]{1,0:T(1,128)}) custom-call(s32[2,128]{1,0:T(2,128)} %bitcast.31, f32[2,128]{1,0:T(2,128)} %bitcast.32, bf16[128,2048]{1,0:T(8,128)(2,1)} %cotan_ref.1, s32[1,56]{1,0:T(1,128)} %bitcast.33), custom_call_target="tpu_custom_call" | custom-call | flops 200000000 | bytes 2000000 | tf_op jit(solution)/shard_map/plan/pallas_call | solution.py:81
  3.7 4.6 %all-to-all-start = ((bf16[8,40,2048]{2,1,0:T(8,128)(2,1)}), bf16[8,40,2048]{2,1,0:T(8,128)(2,1)S(1)}, u32[]{:S(2)}, u32[]{:S(2)}) async-start(bf16[8,40,2048]{2,1,0:T(8,128)(2,1)} %get-tuple-element.22), calls=%async_computation | async-start | bytes 2621440 | tf_op jit(solution)/shard_map/all_to_all | solution.py:305
  8.3 18.7 %all-to-all-done = bf16[8,40,2048]{2,1,0:T(8,128)(2,1)S(1)} async-done(((bf16[8,40,2048]{2,1,0:T(8,128)(2,1)}), bf16[8,40,2048]{2,1,0:T(8,128)(2,1)S(1)}, u32[]{:S(2)}, u32[]{:S(2)}) %all-to-all-start) | async-done | bytes 1310752 | tf_op jit(solution)/shard_map/all_to_all | solution.py:305
  27.0 6.0 %products.2 = (bf16[4,1040,128]{2,1,0:T(8,128)(2,1)S(1)}, bf16[4,1040,128]{2,1,0:T(8,128)(2,1)S(1)}, bf16[4,1040,128]{2,1,0:T(8,128)(2,1)S(1)}, bf16[4,1040,128]{2,1,0:T(8,128)(2,1)S(1)}) custom-call(s32[16,128]{1,0:T(8,128)S(1)} %copy-done.3, s32[2]{0:T(128)S(1)} %pad_add_fusion.place_ref, s32[1,128]{1,0:T(1,128)S(1)} %copy-done.4, ...), custom_call_target="tpu_custom_call" | custom-call | flops 2684354560 | bytes 8200000 | tf_op jit(solution)/shard_map/products/pallas_call | solution.py:154
  33.0 1.6 collective-permute-start
  34.7 2.9 %collective-permute-start.1 = (bf16[4,1040,128]{2,1,0:T(8,128)(2,1)S(1)}, bf16[4,1040,128]{2,1,0:T(8,128)(2,1)S(1)}, u32[]{:S(2)}, u32[]{:S(2)}) collective-permute-start(bf16[4,1040,128]{2,1,0:T(8,128)(2,1)S(1)} %get-tuple-element.25), channel_id=1, source_target_pairs={{0,2},{1,3},{2,0},{3,1},{4,6},{5,7},{6,4},{7,5},{8,10},{9,11},{10,... | collective-permute-start | bytes 3194888 | tf_op jit(solution)/shard_map/ppermute | solution.py:313
  37.6 1.3 collective-permute-start.2
  38.9 2.3 %copy-done = bf16[1,1,8,40,7168]{4,3,2,1,0:T(8,128)(2,1)S(1)} copy-done((bf16[1,1,8,40,7168]{4,3,2,1,0:T(8,128)(2,1)S(1)}, bf16[1,1,8,40,7168]{4,3,2,1,0:T(8,128)(2,1)}, u32[]{:S(2)}) %copy-start) | copy-done | bytes 4587544
  41.2 26.7 %norms.1 = f32[56,1,128]{2,1,0:T(1,128)S(1)} custom-call(bf16[320,7168]{1,0:T(8,128)(2,1)S(1)} %bitcast.19, bf16[320,7168]{1,0:T(8,128)(2,1)S(1)} %bitcast.22, bf16[320,2048]{1,0:T(8,128)(2,1)S(1)} %bitcast.25, bf16[320,2048]{1,0:T(8,128)(2,1)S(1)} %bitcast.28), custom_call_target="tpu_custom_call" | custom-call | flops 18790481920 | bytes 11775040 | tf_op jit(solution)/shard_map/norms/pallas_call | solution.py:198
  67.9 5.6 %products.3 = (bf16[4,1040,128]{2,1,0:T(8,128)(2,1)S(1)}, bf16[4,1040,128]{2,1,0:T(8,128)(2,1)S(1)}, bf16[4,1040,128]{2,1,0:T(8,128)(2,1)S(1)}, bf16[4,1040,128]{2,1,0:T(8,128)(2,1)S(1)}) custom-call(s32[16,128]{1,0:T(8,128)S(1)} %copy-done.3, s32[2]{0:T(128)S(1)} %pad_add_fusion.place_ref, s32[1,128]{1,0:T(1,128)S(1)} %copy-done.4, ...), custom_call_target="tpu_custom_call" | custom-call | flops 2684354560 | bytes 8200000 | tf_op jit(solution)/shard_map/products/pallas_call | solution.py:154
  73.5 2.0 collective-permute-start.3
  75.5 3.6 %collective-permute-start.4 = (bf16[4,1040,128]{2,1,0:T(8,128)(2,1)S(1)}, bf16[4,1040,128]{2,1,0:T(8,128)(2,1)S(1)}, u32[]{:S(2)}, u32[]{:S(2)}) collective-permute-start(bf16[4,1040,128]{2,1,0:T(8,128)(2,1)S(1)} %get-tuple-element.33), channel_id=1, source_target_pairs={{0,8},{1,9},{2,10},{3,11},{4,12},{5,13},{6,14},{7,15},{8,0},{9,1},... | collective-permute-start | bytes 3194888 | tf_op jit(solution)/shard_map/ppermute | solution.py:316
  79.2 1.6 collective-permute-start.5
  80.7 2.6 %collective-permute-done.1.refs_2_ = bf16[4,1040,128]{2,1,0:T(8,128)(2,1)S(1)} collective-permute-done((bf16[4,1040,128]{2,1,0:T(8,128)(2,1)S(1)}, bf16[4,1040,128]{2,1,0:T(8,128)(2,1)S(1)}, u32[]{:S(2)}, u32[]{:S(2)}) %collective-permute-start.1) | collective-permute-done | bytes 1064992 | tf_op jit(solution)/shard_map/ppermute | solution.py:313
  83.6 0.1 pad_maximum_fusion
  83.7 2.0 collective-permute-start.6
  85.8 2.2 %collective-permute-start.7 = (bf16[4,1040,128]{2,1,0:T(8,128)(2,1)S(1)}, bf16[4,1040,128]{2,1,0:T(8,128)(2,1)S(1)}, u32[]{:S(2)}, u32[]{:S(2)}) collective-permute-start(bf16[4,1040,128]{2,1,0:T(8,128)(2,1)S(1)} %pad_maximum_fusion.1), channel_id=1, source_target_pairs={{0,12},{1,13},{2,14},{3,15},{4,0},{5,1},{6,2},{7,3},{8,4},{9,5},{1... | collective-permute-start | bytes 3194888 | tf_op jit(solution)/shard_map/ppermute | solution.py:316
  88.0 37.8 %collective-permute-done.5.refs_7_ = bf16[4,1040,128]{2,1,0:T(8,128)(2,1)S(1)} collective-permute-done((bf16[4,1040,128]{2,1,0:T(8,128)(2,1)S(1)}, bf16[4,1040,128]{2,1,0:T(8,128)(2,1)S(1)}, u32[]{:S(2)}, u32[]{:S(2)}) %collective-permute-start.5) | collective-permute-done | bytes 1064992 | tf_op jit(solution)/shard_map/ppermute | solution.py:316
  125.8 0.5 collective-permute-done.4.refs_6_
  126.6 0.8 collective-permute-start.8
  127.5 2.6 %collective-permute-start.9 = (bf16[4,1040,128]{2,1,0:T(8,128)(2,1)S(1)}, bf16[4,1040,128]{2,1,0:T(8,128)(2,1)S(1)}, u32[]{:S(2)}, u32[]{:S(2)}) collective-permute-start(bf16[4,1040,128]{2,1,0:T(8,128)(2,1)S(1)} %pad_maximum_fusion.3), channel_id=1, source_target_pairs={{0,3},{1,0},{2,1},{3,2},{4,7},{5,4},{6,5},{7,6},{8,11},{9,8},{10,9... | collective-permute-start | bytes 3194888 | tf_op jit(solution)/shard_map/ppermute | solution.py:313
  130.2 2.9 %collective-permute-start.10 = (bf16[4,1040,128]{2,1,0:T(8,128)(2,1)S(1)}, bf16[4,1040,128]{2,1,0:T(8,128)(2,1)S(1)}, u32[]{:S(2)}, u32[]{:S(2)}) collective-permute-start(bf16[4,1040,128]{2,1,0:T(8,128)(2,1)S(1)} %pad_maximum_fusion.4), channel_id=1, source_target_pairs={{0,8},{1,9},{2,10},{3,11},{4,12},{5,13},{6,14},{7,15},{8,0},{9,1},... | collective-permute-start | bytes 3194888 | tf_op jit(solution)/shard_map/ppermute | solution.py:316
  133.3 13.4 %collective-permute-done.6.refs_0_ = bf16[4,1040,128]{2,1,0:T(8,128)(2,1)S(1)} collective-permute-done((bf16[4,1040,128]{2,1,0:T(8,128)(2,1)S(1)}, bf16[4,1040,128]{2,1,0:T(8,128)(2,1)S(1)}, u32[]{:S(2)}, u32[]{:S(2)}) %collective-permute-start.6) | collective-permute-done | bytes 1064992 | tf_op jit(solution)/shard_map/ppermute | solution.py:316
  146.7 0.3 collective-permute-start.11
  147.0 1.9 update.2.base_ref
  148.9 23.4 %collective-permute-done.8.refs_2_ = bf16[4,1040,128]{2,1,0:T(8,128)(2,1)S(1)} collective-permute-done((bf16[4,1040,128]{2,1,0:T(8,128)(2,1)S(1)}, bf16[4,1040,128]{2,1,0:T(8,128)(2,1)S(1)}, u32[]{:S(2)}, u32[]{:S(2)}) %collective-permute-start.8) | collective-permute-done | bytes 1064992 | tf_op jit(solution)/shard_map/ppermute | solution.py:313
  172.3 3.1 %update.3.base_ref = f32[7168,128]{1,0:T(8,128)S(1)} custom-call(f32[7168,128]{1,0:T(8,128)S(1)} %update.2.base_ref, bf16[4,1040,128]{2,1,0:T(8,128)(2,1)S(1)} %collective-permute-done.6.refs_0_, bf16[4,1040,128]{2,1,0:T(8,128)(2,1)S(1)} %collective-permute-done.7.refs_1_, bf16[4,1040,128]{2,1,0:T(8,128)(2,1)S(1)} %collective-permute-done.8.refs_2_, ...), custom_call_target="tpu_custom_call" | custom-call | flops 5000000000 | bytes 16000000 | tf_op jit(solution)/shard_map/update/pallas_call | solution.py:275
  175.5 3.7 %update_last.1 = (f32[7168,128]{1,0:T(8,128)}, f32[16,128]{1,0:T(8,128)}) custom-call(f32[7168,128]{1,0:T(8,128)S(1)} %update.3.base_ref, bf16[4,1040,128]{2,1,0:T(8,128)(2,1)S(1)} %collective-permute-done.10.refs_0_, bf16[4,1040,128]{2,1,0:T(8,128)(2,1)S(1)} %collective-permute-done.11.refs_1_), custom_call_target="tpu_custom_call" | custom-call | flops 5000000000 | bytes 16000000 | tf_op jit(solution)/shard_map/update_last/pallas_call | solution.py:275
  179.2 12.8 %all-to-all-start.1 = ((f32[16,1,128]{2,1,0:T(1,128)}), f32[16,1,128]{2,1,0:T(1,128)S(1)}, u32[]{:S(2)}, u32[]{:S(2)}) async-start(f32[16,1,128]{2,1,0:T(1,128)} %bitcast.12), calls=%async_computation.1 | async-start | bytes 16384 | tf_op jit(solution)/shard_map/all_to_all | solution.py:349
  191.9 0.5 reduce_sum.18
  192.4 6.9 %all-to-all-done.1 = f32[16,1,128]{2,1,0:T(1,128)S(1)} async-done(((f32[16,1,128]{2,1,0:T(1,128)}), f32[16,1,128]{2,1,0:T(1,128)S(1)}, u32[]{:S(2)}, u32[]{:S(2)}) %all-to-all-start.1) | async-done | bytes 8224 | tf_op jit(solution)/shard_map/all_to_all | solution.py:349
  199.4 0.5 subtract_bitcast_fusion
  (36 shorter events, 1.3 us)
Async XLA Ops:
  3.7 23.3 %copy-start.2 = (bf16[1,1,320,2048]{3,2,1,0:T(8,128)(2,1)S(1)}, bf16[1,1,320,2048]{3,2,1,0:T(8,128)(2,1)}, u32[]{:S(2)}) copy-start(bf16[1,1,320,2048]{3,2,1,0:T(8,128)(2,1)} %param.13) | copy-start | bytes 3932164
  3.7 23.3 %copy-start.3 = (s32[16,128]{1,0:T(8,128)S(1)}, s32[16,128]{1,0:T(8,128)}, u32[]{:S(2)}) copy-start(s32[16,128]{1,0:T(8,128)} %get-tuple-element.20.ids_ref) | copy-start | bytes 24580
  3.7 23.3 %copy-start.4 = (s32[1,128]{1,0:T(1,128)S(1)}, s32[1,128]{1,0:T(1,128)}, u32[]{:S(2)}) copy-start(s32[1,128]{1,0:T(1,128)} %get-tuple-element.21.row_ref) | copy-start | bytes 1540
  3.7 35.2 %slice-start = ((s8[4587520]{0:T(1024)(128)(4,1)}), s8[393216]{0:T(1024)(128)(4,1)S(1)}, s32[]{:S(2)}) async-start(s8[4587520]{0:T(1024)(128)(4,1)} %bitcast.17), calls=%async_computation.2 | async-start | bytes 786432
  3.7 23.3 %all-to-all-start = ((bf16[8,40,2048]{2,1,0:T(8,128)(2,1)}), bf16[8,40,2048]{2,1,0:T(8,128)(2,1)S(1)}, u32[]{:S(2)}, u32[]{:S(2)}) async-start(bf16[8,40,2048]{2,1,0:T(8,128)(2,1)} %get-tuple-element.22), calls=%async_computation | async-start | bytes 2621440 | tf_op jit(solution)/shard_map/all_to_all | solution.py:305
  27.0 11.9 %slice-start.1 = ((s8[4587520]{0:T(1024)(128)(4,1)}), s8[4194304]{0:T(1024)(128)(4,1)S(1)}, s32[]{:S(2)}) async-start(s8[4587520]{0:T(1024)(128)(4,1)} %bitcast.17), calls=%async_computation.3 | async-start | bytes 8388608
  33.0 46.1 %collective-permute-start = (bf16[4,1040,128]{2,1,0:T(8,128)(2,1)S(1)}, bf16[4,1040,128]{2,1,0:T(8,128)(2,1)S(1)}, u32[]{:S(2)}, u32[]{:S(2)}) collective-permute-start(bf16[4,1040,128]{2,1,0:T(8,128)(2,1)S(1)} %get-tuple-element.24), channel_id=1, source_target_pairs={{0,1},{1,2},{2,3},{3,0},{4,5},{5,6},{6,7},{7,4},{8,9},{9,10},{10,1... | collective-permute-start | bytes 3194888 | tf_op jit(solution)/shard_map/ppermute | solution.py:313
  34.7 48.6 %collective-permute-start.1 = (bf16[4,1040,128]{2,1,0:T(8,128)(2,1)S(1)}, bf16[4,1040,128]{2,1,0:T(8,128)(2,1)S(1)}, u32[]{:S(2)}, u32[]{:S(2)}) collective-permute-start(bf16[4,1040,128]{2,1,0:T(8,128)(2,1)S(1)} %get-tuple-element.25), channel_id=1, source_target_pairs={{0,2},{1,3},{2,0},{3,1},{4,6},{5,7},{6,4},{7,5},{8,10},{9,11},{10,... | collective-permute-start | bytes 3194888 | tf_op jit(solution)/shard_map/ppermute | solution.py:313
  37.6 45.8 %collective-permute-start.2 = (bf16[4,1040,128]{2,1,0:T(8,128)(2,1)S(1)}, bf16[4,1040,128]{2,1,0:T(8,128)(2,1)S(1)}, u32[]{:S(2)}, u32[]{:S(2)}) collective-permute-start(bf16[4,1040,128]{2,1,0:T(8,128)(2,1)S(1)} %get-tuple-element.26), channel_id=1, source_target_pairs={{0,3},{1,0},{2,1},{3,2},{4,7},{5,4},{6,5},{7,6},{8,11},{9,8},{10,9... | collective-permute-start | bytes 3194888 | tf_op jit(solution)/shard_map/ppermute | solution.py:313
  38.9 2.3 %copy-start = (bf16[1,1,8,40,7168]{4,3,2,1,0:T(8,128)(2,1)S(1)}, bf16[1,1,8,40,7168]{4,3,2,1,0:T(8,128)(2,1)}, u32[]{:S(2)}) copy-start(bf16[1,1,8,40,7168]{4,3,2,1,0:T(8,128)(2,1)} %param.12) | copy-start | bytes 13762564
  41.2 26.7 %copy-start.1 = (bf16[1,1,8,40,7168]{4,3,2,1,0:T(8,128)(2,1)S(1)}, bf16[1,1,8,40,7168]{4,3,2,1,0:T(8,128)(2,1)}, u32[]{:S(2)}) copy-start(bf16[1,1,8,40,7168]{4,3,2,1,0:T(8,128)(2,1)} %param.12) | copy-start | bytes 13762564
  73.5 52.8 %collective-permute-start.3 = (bf16[4,1040,128]{2,1,0:T(8,128)(2,1)S(1)}, bf16[4,1040,128]{2,1,0:T(8,128)(2,1)S(1)}, u32[]{:S(2)}, u32[]{:S(2)}) collective-permute-start(bf16[4,1040,128]{2,1,0:T(8,128)(2,1)S(1)} %get-tuple-element.32), channel_id=1, source_target_pairs={{0,4},{1,5},{2,6},{3,7},{4,8},{5,9},{6,10},{7,11},{8,12},{9,13},{1... | collective-permute-start | bytes 3194888 | tf_op jit(solution)/shard_map/ppermute | solution.py:316
  75.5 50.8 %collective-permute-start.4 = (bf16[4,1040,128]{2,1,0:T(8,128)(2,1)S(1)}, bf16[4,1040,128]{2,1,0:T(8,128)(2,1)S(1)}, u32[]{:S(2)}, u32[]{:S(2)}) collective-permute-start(bf16[4,1040,128]{2,1,0:T(8,128)(2,1)S(1)} %get-tuple-element.33), channel_id=1, source_target_pairs={{0,8},{1,9},{2,10},{3,11},{4,12},{5,13},{6,14},{7,15},{8,0},{9,1},... | collective-permute-start | bytes 3194888 | tf_op jit(solution)/shard_map/ppermute | solution.py:316
  79.2 46.6 %collective-permute-start.5 = (bf16[4,1040,128]{2,1,0:T(8,128)(2,1)S(1)}, bf16[4,1040,128]{2,1,0:T(8,128)(2,1)S(1)}, u32[]{:S(2)}, u32[]{:S(2)}) collective-permute-start(bf16[4,1040,128]{2,1,0:T(8,128)(2,1)S(1)} %get-tuple-element.34), channel_id=1, source_target_pairs={{0,12},{1,13},{2,14},{3,15},{4,0},{5,1},{6,2},{7,3},{8,4},{9,5},{1... | collective-permute-start | bytes 3194888 | tf_op jit(solution)/shard_map/ppermute | solution.py:316
  83.7 63.0 %collective-permute-start.6 = (bf16[4,1040,128]{2,1,0:T(8,128)(2,1)S(1)}, bf16[4,1040,128]{2,1,0:T(8,128)(2,1)S(1)}, u32[]{:S(2)}, u32[]{:S(2)}) collective-permute-start(bf16[4,1040,128]{2,1,0:T(8,128)(2,1)S(1)} %pad_maximum_fusion), channel_id=1, source_target_pairs={{0,4},{1,5},{2,6},{3,7},{4,8},{5,9},{6,10},{7,11},{8,12},{9,13},{1... | collective-permute-start | bytes 3194888 | tf_op jit(solution)/shard_map/ppermute | solution.py:316
  85.8 63.1 %collective-permute-start.7 = (bf16[4,1040,128]{2,1,0:T(8,128)(2,1)S(1)}, bf16[4,1040,128]{2,1,0:T(8,128)(2,1)S(1)}, u32[]{:S(2)}, u32[]{:S(2)}) collective-permute-start(bf16[4,1040,128]{2,1,0:T(8,128)(2,1)S(1)} %pad_maximum_fusion.1), channel_id=1, source_target_pairs={{0,12},{1,13},{2,14},{3,15},{4,0},{5,1},{6,2},{7,3},{8,4},{9,5},{1... | collective-permute-start | bytes 3194888 | tf_op jit(solution)/shard_map/ppermute | solution.py:316
  126.6 45.8 %collective-permute-start.8 = (bf16[4,1040,128]{2,1,0:T(8,128)(2,1)S(1)}, bf16[4,1040,128]{2,1,0:T(8,128)(2,1)S(1)}, u32[]{:S(2)}, u32[]{:S(2)}) collective-permute-start(bf16[4,1040,128]{2,1,0:T(8,128)(2,1)S(1)} %pad_maximum_fusion.2), channel_id=1, source_target_pairs={{0,1},{1,2},{2,3},{3,0},{4,5},{5,6},{6,7},{7,4},{8,9},{9,10},{10,1... | collective-permute-start | bytes 3194888 | tf_op jit(solution)/shard_map/ppermute | solution.py:313
  127.5 44.9 %collective-permute-start.9 = (bf16[4,1040,128]{2,1,0:T(8,128)(2,1)S(1)}, bf16[4,1040,128]{2,1,0:T(8,128)(2,1)S(1)}, u32[]{:S(2)}, u32[]{:S(2)}) collective-permute-start(bf16[4,1040,128]{2,1,0:T(8,128)(2,1)S(1)} %pad_maximum_fusion.3), channel_id=1, source_target_pairs={{0,3},{1,0},{2,1},{3,2},{4,7},{5,4},{6,5},{7,6},{8,11},{9,8},{10,9... | collective-permute-start | bytes 3194888 | tf_op jit(solution)/shard_map/ppermute | solution.py:313
  130.1 16.9 %copy-start.5 = (f32[1,7168,128]{2,1,0:T(8,128)S(1)}, f32[1,7168,128]{2,1,0:T(8,128)}, u32[]{:S(2)}) copy-start(f32[1,7168,128]{2,1,0:T(8,128)} %param.15) | copy-start | bytes 11010052
  130.2 45.2 %collective-permute-start.10 = (bf16[4,1040,128]{2,1,0:T(8,128)(2,1)S(1)}, bf16[4,1040,128]{2,1,0:T(8,128)(2,1)S(1)}, u32[]{:S(2)}, u32[]{:S(2)}) collective-permute-start(bf16[4,1040,128]{2,1,0:T(8,128)(2,1)S(1)} %pad_maximum_fusion.4), channel_id=1, source_target_pairs={{0,8},{1,9},{2,10},{3,11},{4,12},{5,13},{6,14},{7,15},{8,0},{9,1},... | collective-permute-start | bytes 3194888 | tf_op jit(solution)/shard_map/ppermute | solution.py:316
  146.7 28.8 %collective-permute-start.11 = (bf16[4,1040,128]{2,1,0:T(8,128)(2,1)S(1)}, bf16[4,1040,128]{2,1,0:T(8,128)(2,1)S(1)}, u32[]{:S(2)}, u32[]{:S(2)}) collective-permute-start(bf16[4,1040,128]{2,1,0:T(8,128)(2,1)S(1)} %pad_maximum_fusion.5), channel_id=1, source_target_pairs={{0,2},{1,3},{2,0},{3,1},{4,6},{5,7},{6,4},{7,5},{8,10},{9,11},{10,... | collective-permute-start | bytes 3194888 | tf_op jit(solution)/shard_map/ppermute | solution.py:313
  179.2 20.2 %all-to-all-start.1 = ((f32[16,1,128]{2,1,0:T(1,128)}), f32[16,1,128]{2,1,0:T(1,128)S(1)}, u32[]{:S(2)}, u32[]{:S(2)}) async-start(f32[16,1,128]{2,1,0:T(1,128)} %bitcast.12), calls=%async_computation.1 | async-start | bytes 16384 | tf_op jit(solution)/shard_map/all_to_all | solution.py:349

commit v2 on v1

--- a/solution.py
+++ b/solution.py
@@ -104,8 +104,8 @@
 
 
 def products_kernel(start, count, z_first, ids_ref, place_ref, row_ref, now_hbm, prev_hbm, slots_ref, cotan_ref, *refs):
-    out_refs = refs[0:SIDE]
-    left_ref, right_ref, now_sems, prev_sems = refs[SIDE:]
+    own_refs, far_refs = refs[0:SIDE], (None, *refs[SIDE : 2 * SIDE - 1])
+    left_ref, right_ref, now_sems, prev_sems = refs[2 * SIDE - 1 :]
     rows = slots_ref.shape[0]
     copies = []
     for j in range(count):
@@ -124,9 +124,11 @@
             right_ref[0:rows, at] = slots_ref[:, come]
             right_ref[rows:, at] = -cotan_ref[:, come]
     row = jnp.broadcast_to(row_ref[...].astype(jnp.float32), (TAIL, LANES)).astype(jnp.bfloat16)
-    for out_ref in out_refs:
-        for s in range(SIDE):
-            out_ref[s, count * BLOCK : count * BLOCK + TAIL, :] = row
+    behind = slice(count * BLOCK, count * BLOCK + TAIL)
+    for k in range(SIDE):
+        own_refs[k][0, behind, :] = row
+        for m in range(1, SIDE):
+            far_refs[m][k, behind, :] = row
     for g in range(count // GROUP):
         for copy in copies[2 * g * GROUP : 2 * (g + 1) * GROUP]:
             copy.wait()
@@ -140,10 +142,11 @@
             )
             for s in range(SIDE):
                 piece = acc[:, s * LANES : (s + 1) * LANES].astype(jnp.bfloat16)
-                if z_first:
-                    out_refs[t][s, at, :] = piece
+                first, second = (t, s) if z_first else (s, t)
+                if first == 0:
+                    own_refs[second][0, at, :] = piece
                 else:
-                    out_refs[s][t, at, :] = piece
+                    far_refs[first][second, at, :] = piece
 
 
 def products(ids, place, row, now, prev, slots, cotan, start, count, z_first):
@@ -153,9 +156,10 @@
     hbm = pl.BlockSpec(memory_space=pltpu.HBM)
     return pl.pallas_call(
         functools.partial(products_kernel, start, count, z_first),
-        out_shape=[jax.ShapeDtypeStruct((SIDE, count * BLOCK + TAIL, LANES), jnp.bfloat16)] * SIDE,
+        out_shape=[jax.ShapeDtypeStruct((1, count * BLOCK + TAIL, LANES), jnp.bfloat16)] * SIDE
+        + [jax.ShapeDtypeStruct((SIDE, count * BLOCK + TAIL, LANES), jnp.bfloat16)] * (SIDE - 1),
         in_specs=[smem, smem, vmem, hbm, hbm, vmem, vmem],
-        out_specs=[vmem] * SIDE,
+        out_specs=[vmem] * (2 * SIDE - 1),
         scratch_shapes=[
             pltpu.VMEM((2 * rows, count * BLOCK), jnp.bfloat16),
             pltpu.VMEM((2 * rows, DW), jnp.bfloat16),
@@ -315,36 +319,44 @@
     def along_z(x, k):
         return lax.ppermute(x, "dp", shift(workers, k, 0))
 
-    sent_a = products(ids, place, ids_row, now, prev, slots, cotan, 0, HALF, False)
-    first_a, first_b = {0: sent_a[0]}, {}
-    for k in ORDER:
-        first_a[k] = along_y(sent_a[k], k)
-    sent_b = products(ids, place, ids_row, now, prev, slots, cotan, HALF, HALF, True)
-    first_b[0] = sent_b[0]
-    for k in ORDER:
-        first_b[k] = along_z(sent_b[k], k)
+    def stage_one(start, z_first, near, far):
+        sent = products(ids, place, ids_row, now, prev, slots, cotan, start, HALF, z_first)
+        own, relay = {0: sent[0]}, {}
+        for k in ORDER:
+            relay[k] = near(sent[SIDE - 1 + k], k)
+        for k in ORDER:
+            own[k] = far(sent[k], k)
+        return own, relay
+
+    def stage_two(relay, far):
+        got = {}
+        for k in ORDER:
+            got[k] = far(jnp.stack([relay[j][k] for j in range(1, SIDE)]), k)
+        return got
+
+    own_a, relay_a = stage_one(0, False, along_y, along_z)
+    own_b, relay_b = stage_one(HALF, True, along_z, along_y)
     squared = norms(now, prev, slots, cotan)
-    first_a, squared = lax.optimization_barrier((first_a, squared))
-    second_a, second_b = {}, {}
-    for k in ORDER:
-        second_a[k] = along_z(jnp.stack([first_a[j][k] for j in range(SIDE)]), k)
-    for k in ORDER:
-        second_b[k] = along_y(jnp.stack([first_b[j][k] for j in range(SIDE)]), k)
+    relay_a, squared = lax.optimization_barrier((relay_a, squared))
+    second_a = stage_two(relay_a, along_z)
+    second_b = stage_two(relay_b, along_y)
     diff_norms = jnp.sum(squared, axis=(1, 2)) / (BLOCK * DW)
+    near_a = [own_a[k] for k in range(SIDE)] + [relay_a[k] for k in ORDER]
+    near_b = [own_b[k] for k in range(SIDE)] + [relay_b[k] for k in ORDER]
     (current,) = update(
         stale_sum.reshape(FFW, columns),
-        [first_a[k] for k in range(SIDE)] + [first_b[k] for k in range(SIDE)],
-        [(1, 0)] * SIDE + [(1, HALF)] * SIDE,
+        near_a + near_b,
+        [(1, 0)] * len(near_a) + [(1, HALF)] * len(near_b),
         False,
     )
     (current,) = update(
         current,
         [second_a[k] for k in ORDER[:2]] + [second_b[k] for k in ORDER[:2]],
-        [(SIDE, 0)] * 2 + [(SIDE, HALF)] * 2,
+        [(SIDE - 1, 0)] * 2 + [(SIDE - 1, HALF)] * 2,
         False,
     )
     current, squares = update(
-        current, [second_a[ORDER[2]], second_b[ORDER[2]]], [(SIDE, 0), (SIDE, HALF)], True
+        current, [second_a[ORDER[2]], second_b[ORDER[2]]], [(SIDE - 1, 0), (SIDE - 1, HALF)], True
     )
     everyone = exchange(squares.reshape(workers, 1, LANES), "dp").reshape(workers, LANES)
     norm_totals = jnp.sum(everyone, axis=0)[:BLOCKS] / (BLOCK * DW)

time: 200 us -> 193 us (0.965)
  waiting for transfers between devices: 103 us -> 85.3 us
  starting transfers between devices: 41.1 us -> 52.1 us
    ppermute x6 -> x9, waiting for transfers between devices: 51.6 us -> 33.5 us  [along_z(): return lax.ppermute(x, 'dp', shift(workers, k, 0))]
    ppermute x6 -> x9, starting transfers between devices: 9.61 us -> 16.5 us  [along_y(): return lax.ppermute(x, 'dp', shift(workers, 0, k))]
    all_to_all x1, starting transfers between devices: 12.8 us -> 15.8 us  [local(): exchange(squares.reshape(workers, 1, LANES), 'dp').reshape(workers, LANES)]
    ppermute x6 -> x9, starting transfers between devices: 14.2 us -> 15.3 us  [along_z(): return lax.ppermute(x, 'dp', shift(workers, k, 0))]
    ppermute x6 -> x9, waiting for transfers between devices: 26.1 us -> 26 us  [along_y(): return lax.ppermute(x, 'dp', shift(workers, 0, k))]
  transfers between devices with their start and end apart: 14 -> 20, of which waited for: 7 -> 12; matrix products, arithmetic and copies ran while one was open for 1% -> 1% of each run, Pallas kernels for 19% -> 17%
where the time goes in v2:
time: 193 us
  waiting for transfers between devices  85.3 us (44%)
  starting transfers between devices  52.1 us (27%)
  Pallas kernels  50.1 us (26%)
  local copies, waits for them, and re-layouts  2.66 us (1%)
    ppermute x9, waiting for transfers between devices, along_z(): return lax.ppermute(x, 'dp', shift(workers, k, 0))  33.5 us
    pallas_call x1, Pallas kernels, norms(): pl.pallas_call(norms_kernel, out_shape=jax.ShapeDtypeStruct((BLOCKS, 1, L...  26.7 us
    ppermute x9, waiting for transfers between devices, along_y(): return lax.ppermute(x, 'dp', shift(workers, 0, k))  26 us
    all_to_all x1, waiting for transfers between devices, local(): slots = exchange(table, 'expert').reshape(-1, DW)  18.7 us
    ppermute x9, starting transfers between devices, along_y(): return lax.ppermute(x, 'dp', shift(workers, 0, k))  16.5 us
    all_to_all x1, starting transfers between devices, local(): exchange(squares.reshape(workers, 1, LANES), 'dp').reshape(workers, LANES)  15.8 us
    ppermute x9, starting transfers between devices, along_z(): return lax.ppermute(x, 'dp', shift(workers, k, 0))  15.3 us
    pallas_call x2, Pallas kernels, products(): pl.pallas_call(functools.partial(products_kernel, start, count, z_first),...  11.6 us
  transfers between devices with their start and end apart: 20, of which 12 were waited for; matrix products, arithmetic and copies ran while one was open for 1% of the time, Pallas kernels for 17%

profile of v2, /device:TPU:0, one launch (start us, length us, event | category | flops | bytes accessed | tf_op | source)
XLA Modules:
  0.0 192.7 jit_solution(16238754592819810300)
XLA Ops:
  0.6 3.0 %plan.1 = (bf16[8,40,2048]{2,1,0:T(8,128)(2,1)}, s32[16,128]{1,0:T(8,128)}, s32[1,128]{1,0:T(1,128)}) custom-call(s32[2,128]{1,0:T(2,128)} %bitcast.33, f32[2,128]{1,0:T(2,128)} %bitcast.34, bf16[128,2048]{1,0:T(8,128)(2,1)} %cotan_ref.1, s32[1,56]{1,0:T(1,128)} %bitcast.35), custom_call_target="tpu_custom_call" | custom-call | flops 200000000 | bytes 2000000 | tf_op jit(solution)/shard_map/plan/pallas_call | solution.py:81
  3.7 4.6 %all-to-all-start = ((bf16[8,40,2048]{2,1,0:T(8,128)(2,1)}), bf16[8,40,2048]{2,1,0:T(8,128)(2,1)S(1)}, u32[]{:S(2)}, u32[]{:S(2)}) async-start(bf16[8,40,2048]{2,1,0:T(8,128)(2,1)} %get-tuple-element.27), calls=%async_computation | async-start | bytes 2621440 | tf_op jit(solution)/shard_map/all_to_all | solution.py:309
  8.3 18.7 %all-to-all-done = bf16[8,40,2048]{2,1,0:T(8,128)(2,1)S(1)} async-done(((bf16[8,40,2048]{2,1,0:T(8,128)(2,1)}), bf16[8,40,2048]{2,1,0:T(8,128)(2,1)S(1)}, u32[]{:S(2)}, u32[]{:S(2)}) %all-to-all-start) | async-done | bytes 1310752 | tf_op jit(solution)/shard_map/all_to_all | solution.py:309
  27.0 6.0 %products.2 = (bf16[1,1040,128]{2,1,0:T(8,128)(2,1)S(1)}, bf16[1,1040,128]{2,1,0:T(8,128)(2,1)S(1)}, bf16[1,1040,128]{2,1,0:T(8,128)(2,1)S(1)}, bf16[1,1040,128]...) custom-call(s32[16,128]{1,0:T(8,128)S(1)} %copy-done.2, ...), custom_call_target="tpu_custom_call" | custom-call | flops 2684354560 | bytes 8200000 | tf_op jit(solution)/shard_map/products/pallas_call | solution.py:157
  33.1 2.3 %copy-done = bf16[1,1,8,40,7168]{4,3,2,1,0:T(8,128)(2,1)S(1)} copy-done((bf16[1,1,8,40,7168]{4,3,2,1,0:T(8,128)(2,1)S(1)}, bf16[1,1,8,40,7168]{4,3,2,1,0:T(8,128)(2,1)}, u32[]{:S(2)}) %copy-start) | copy-done | bytes 4587544
  35.4 5.6 %products.3 = (bf16[1,1040,128]{2,1,0:T(8,128)(2,1)S(1)}, bf16[1,1040,128]{2,1,0:T(8,128)(2,1)S(1)}, bf16[1,1040,128]{2,1,0:T(8,128)(2,1)S(1)}, bf16[1,1040,128]...) custom-call(s32[16,128]{1,0:T(8,128)S(1)} %copy-done.2, ...), custom_call_target="tpu_custom_call" | custom-call | flops 2684354560 | bytes 8200000 | tf_op jit(solution)/shard_map/products/pallas_call | solution.py:157
  41.0 1.6 collective-permute-start.3
  42.6 2.9 %collective-permute-start.4 = (bf16[4,1040,128]{2,1,0:T(8,128)(2,1)S(1)}, bf16[4,1040,128]{2,1,0:T(8,128)(2,1)S(1)}, u32[]{:S(2)}, u32[]{:S(2)}) collective-permute-start(bf16[4,1040,128]{2,1,0:T(8,128)(2,1)S(1)} %get-tuple-element.33), channel_id=1, source_target_pairs={{0,2},{1,3},{2,0},{3,1},{4,6},{5,7},{6,4},{7,5},{8,10},{9,11},{10,... | collective-permute-start | bytes 3194888 | tf_op jit(solution)/shard_map/ppermute | solution.py:317
  45.5 1.3 collective-permute-start.5
  46.9 4.0 %collective-permute-start.10 = (bf16[4,1040,128]{2,1,0:T(8,128)(2,1)S(1)}, bf16[4,1040,128]{2,1,0:T(8,128)(2,1)S(1)}, u32[]{:S(2)}, u32[]{:S(2)}) collective-permute-start(bf16[4,1040,128]{2,1,0:T(8,128)(2,1)S(1)} %get-tuple-element.43), channel_id=1, source_target_pairs={{0,12},{1,13},{2,14},{3,15},{4,0},{5,1},{6,2},{7,3},{8,4},{9,5},{1... | collective-permute-start | bytes 3194888 | tf_op jit(solution)/shard_map/ppermute | solution.py:320
  50.9 26.7 %norms.1 = f32[56,1,128]{2,1,0:T(1,128)S(1)} custom-call(bf16[320,7168]{1,0:T(8,128)(2,1)S(1)} %bitcast.20, bf16[320,7168]{1,0:T(8,128)(2,1)S(1)} %bitcast.25, bf16[320,2048]{1,0:T(8,128)(2,1)S(1)} %bitcast.28, bf16[320,2048]{1,0:T(8,128)(2,1)S(1)} %bitcast.31), custom_call_target="tpu_custom_call" | custom-call | flops 18790481920 | bytes 11775040 | tf_op jit(solution)/shard_map/norms/pallas_call | solution.py:202
  77.6 1.3 collective-permute-start
  78.9 12.3 %collective-permute-done.4.refs_6_ = bf16[4,1040,128]{2,1,0:T(8,128)(2,1)S(1)} collective-permute-done((bf16[4,1040,128]{2,1,0:T(8,128)(2,1)S(1)}, bf16[4,1040,128]{2,1,0:T(8,128)(2,1)S(1)}, u32[]{:S(2)}, u32[]{:S(2)}) %collective-permute-start.4) | collective-permute-done | bytes 1064992 | tf_op jit(solution)/shard_map/ppermute | solution.py:317
  91.3 3.9 %collective-permute-start.1 = (bf16[1,1040,128]{2,1,0:T(8,128)(2,1)S(1)}, bf16[1,1040,128]{2,1,0:T(8,128)(2,1)S(1)}, u32[]{:S(2)}, u32[]{:S(2)}) collective-permute-start(bf16[1,1040,128]{2,1,0:T(8,128)(2,1)S(1)} %get-tuple-element.30), channel_id=1, source_target_pairs={{0,8},{1,9},{2,10},{3,11},{4,12},{5,13},{6,14},{7,15},{8,0},{9,1},... | collective-permute-start | bytes 798728 | tf_op jit(solution)/shard_map/ppermute | solution.py:320
  95.9 5.4 %collective-permute-done.10.refs_12_ = bf16[4,1040,128]{2,1,0:T(8,128)(2,1)S(1)} collective-permute-done((bf16[4,1040,128]{2,1,0:T(8,128)(2,1)S(1)}, bf16[4,1040,128]{2,1,0:T(8,128)(2,1)S(1)}, u32[]{:S(2)}, u32[]{:S(2)}) %collective-permute-start.10) | collective-permute-done | bytes 1064992 | tf_op jit(solution)/shard_map/ppermute | solution.py:320
  101.3 2.8 %collective-permute-start.6 = (bf16[1,1040,128]{2,1,0:T(8,128)(2,1)S(1)}, bf16[1,1040,128]{2,1,0:T(8,128)(2,1)S(1)}, u32[]{:S(2)}, u32[]{:S(2)}) collective-permute-start(bf16[1,1040,128]{2,1,0:T(8,128)(2,1)S(1)} %get-tuple-element.39), channel_id=1, source_target_pairs={{0,1},{1,2},{2,3},{3,0},{4,5},{5,6},{6,7},{7,4},{8,9},{9,10},{10,1... | collective-permute-start | bytes 798728 | tf_op jit(solution)/shard_map/ppermute | solution.py:317
  104.3 18.9 %collective-permute-done.9.refs_11_ = bf16[4,1040,128]{2,1,0:T(8,128)(2,1)S(1)} collective-permute-done((bf16[4,1040,128]{2,1,0:T(8,128)(2,1)S(1)}, bf16[4,1040,128]{2,1,0:T(8,128)(2,1)S(1)}, u32[]{:S(2)}, u32[]{:S(2)}) %collective-permute-start.9) | collective-permute-done | bytes 1064992 | tf_op jit(solution)/shard_map/ppermute | solution.py:320
  123.3 3.5 %collective-permute-start.7 = (bf16[1,1040,128]{2,1,0:T(8,128)(2,1)S(1)}, bf16[1,1040,128]{2,1,0:T(8,128)(2,1)S(1)}, u32[]{:S(2)}, u32[]{:S(2)}) collective-permute-start(bf16[1,1040,128]{2,1,0:T(8,128)(2,1)S(1)} %get-tuple-element.40), channel_id=1, source_target_pairs={{0,2},{1,3},{2,0},{3,1},{4,6},{5,7},{6,4},{7,5},{8,10},{9,11},{10,... | collective-permute-start | bytes 798728 | tf_op jit(solution)/shard_map/ppermute | solution.py:317
  127.0 1.8 collective-permute-start.12
  129.1 3.0 %collective-permute-start.13 = (bf16[3,1040,128]{2,1,0:T(8,128)(2,1)S(1)}, bf16[3,1040,128]{2,1,0:T(8,128)(2,1)S(1)}, u32[]{:S(2)}, u32[]{:S(2)}) collective-permute-start(bf16[3,1040,128]{2,1,0:T(8,128)(2,1)S(1)} %pad_maximum_fusion.1), channel_id=1, source_target_pairs={{0,12},{1,13},{2,14},{3,15},{4,0},{5,1},{6,2},{7,3},{8,4},{9,5},{1... | collective-permute-start | bytes 2396168 | tf_op jit(solution)/shard_map/ppermute | solution.py:320
  133.5 3.6 %collective-permute-start.15 = (bf16[3,1040,128]{2,1,0:T(8,128)(2,1)S(1)}, bf16[3,1040,128]{2,1,0:T(8,128)(2,1)S(1)}, u32[]{:S(2)}, u32[]{:S(2)}) collective-permute-start(bf16[3,1040,128]{2,1,0:T(8,128)(2,1)S(1)} %pad_maximum_fusion.3), channel_id=1, source_target_pairs={{0,3},{1,0},{2,1},{3,2},{4,7},{5,4},{6,5},{7,6},{8,11},{9,8},{10,9... | collective-permute-start | bytes 2396168 | tf_op jit(solution)/shard_map/ppermute | solution.py:317
  137.4 2.8 %collective-permute-done.8.refs_10_ = bf16[1,1040,128]{2,1,0:T(8,128)(2,1)S(1)} collective-permute-done((bf16[1,1040,128]{2,1,0:T(8,128)(2,1)S(1)}, bf16[1,1040,128]{2,1,0:T(8,128)(2,1)S(1)}, u32[]{:S(2)}, u32[]{:S(2)}) %collective-permute-start.8) | collective-permute-done | bytes 266272 | tf_op jit(solution)/shard_map/ppermute | solution.py:317
  140.8 6.3 %collective-permute-done.12.refs_0_ = bf16[3,1040,128]{2,1,0:T(8,128)(2,1)S(1)} collective-permute-done((bf16[3,1040,128]{2,1,0:T(8,128)(2,1)S(1)}, bf16[3,1040,128]{2,1,0:T(8,128)(2,1)S(1)}, u32[]{:S(2)}, u32[]{:S(2)}) %collective-permute-start.12) | collective-permute-done | bytes 798752 | tf_op jit(solution)/shard_map/ppermute | solution.py:320
  147.1 2.9 %update.2.base_ref = f32[7168,128]{1,0:T(8,128)S(1)} custom-call(f32[7168,128]{1,0:T(8,128)S(1)} %bitcast.32, bf16[1,1040,128]{2,1,0:T(8,128)(2,1)S(1)} %get-tuple-element.28.refs_0_, bf16[1,1040,128]{2,1,0:T(8,128)(2,1)S(1)} %collective-permute-done.refs_1_, bf16[1,1040,128]{2,1,0:T(8,128)(2,1)S(1)} %collective-permute-done.1.refs_2_, ...), custom_call_target="tpu_custom_call" | custom-call | flops 5000000000 | bytes 16000000 | tf_op jit(solution)/shard_map/update/pallas_call | solution.py:279
  150.1 2.3 %collective-permute-done.14.refs_2_ = bf16[3,1040,128]{2,1,0:T(8,128)(2,1)S(1)} collective-permute-done((bf16[3,1040,128]{2,1,0:T(8,128)(2,1)S(1)}, bf16[3,1040,128]{2,1,0:T(8,128)(2,1)S(1)}, u32[]{:S(2)}, u32[]{:S(2)}) %collective-permute-start.14) | collective-permute-done | bytes 798752 | tf_op jit(solution)/shard_map/ppermute | solution.py:317
  152.3 5.0 %collective-permute-done.15.refs_3_ = bf16[3,1040,128]{2,1,0:T(8,128)(2,1)S(1)} collective-permute-done((bf16[3,1040,128]{2,1,0:T(8,128)(2,1)S(1)}, bf16[3,1040,128]{2,1,0:T(8,128)(2,1)S(1)}, u32[]{:S(2)}, u32[]{:S(2)}) %collective-permute-start.15) | collective-permute-done | bytes 798752 | tf_op jit(solution)/shard_map/ppermute | solution.py:317
  157.3 2.4 %update.3.base_ref = f32[7168,128]{1,0:T(8,128)S(1)} custom-call(f32[7168,128]{1,0:T(8,128)S(1)} %update.2.base_ref, bf16[3,1040,128]{2,1,0:T(8,128)(2,1)S(1)} %collective-permute-done.12.refs_0_, bf16[3,1040,128]{2,1,0:T(8,128)(2,1)S(1)} %collective-permute-done.13.refs_1_, bf16[3,1040,128]{2,1,0:T(8,128)(2,1)S(1)} %collective-permute-done.14.refs_2_, ...), custom_call_target="tpu_custom_call" | custom-call | flops 5000000000 | bytes 16000000 | tf_op jit(solution)/shard_map/update/pallas_call | solution.py:279
  159.8 3.0 %collective-permute-done.16.refs_0_ = bf16[3,1040,128]{2,1,0:T(8,128)(2,1)S(1)} collective-permute-done((bf16[3,1040,128]{2,1,0:T(8,128)(2,1)S(1)}, bf16[3,1040,128]{2,1,0:T(8,128)(2,1)S(1)}, u32[]{:S(2)}, u32[]{:S(2)}) %collective-permute-start.16) | collective-permute-done | bytes 798752 | tf_op jit(solution)/shard_map/ppermute | solution.py:320
  162.8 2.6 %collective-permute-done.17.refs_1_ = bf16[3,1040,128]{2,1,0:T(8,128)(2,1)S(1)} collective-permute-done((bf16[3,1040,128]{2,1,0:T(8,128)(2,1)S(1)}, bf16[3,1040,128]{2,1,0:T(8,128)(2,1)S(1)}, u32[]{:S(2)}, u32[]{:S(2)}) %collective-permute-start.17) | collective-permute-done | bytes 798752 | tf_op jit(solution)/shard_map/ppermute | solution.py:317
  165.4 3.3 %update_last.1 = (f32[7168,128]{1,0:T(8,128)}, f32[16,128]{1,0:T(8,128)}) custom-call(f32[7168,128]{1,0:T(8,128)S(1)} %update.3.base_ref, bf16[3,1040,128]{2,1,0:T(8,128)(2,1)S(1)} %collective-permute-done.16.refs_0_, bf16[3,1040,128]{2,1,0:T(8,128)(2,1)S(1)} %collective-permute-done.17.refs_1_), custom_call_target="tpu_custom_call" | custom-call | flops 5000000000 | bytes 16000000 | tf_op jit(solution)/shard_map/update_last/pallas_call | solution.py:279
  168.8 15.8 %all-to-all-start.1 = ((f32[16,1,128]{2,1,0:T(1,128)}), f32[16,1,128]{2,1,0:T(1,128)S(1)}, u32[]{:S(2)}, u32[]{:S(2)}) async-start(f32[16,1,128]{2,1,0:T(1,128)} %bitcast.12), calls=%async_computation.1 | async-start | bytes 16384 | tf_op jit(solution)/shard_map/all_to_all | solution.py:361
  185.1 7.1 %all-to-all-done.1 = f32[16,1,128]{2,1,0:T(1,128)S(1)} async-done(((f32[16,1,128]{2,1,0:T(1,128)}), f32[16,1,128]{2,1,0:T(1,128)S(1)}, u32[]{:S(2)}, u32[]{:S(2)}) %all-to-all-start.1) | async-done | bytes 8224 | tf_op jit(solution)/shard_map/all_to_all | solution.py:361
  (50 shorter events, 4.9 us)
Async XLA Ops:
  3.7 23.3 %copy-start.1 = (bf16[1,1,320,2048]{3,2,1,0:T(8,128)(2,1)S(1)}, bf16[1,1,320,2048]{3,2,1,0:T(8,128)(2,1)}, u32[]{:S(2)}) copy-start(bf16[1,1,320,2048]{3,2,1,0:T(8,128)(2,1)} %param.13) | copy-start | bytes 3932164
  3.7 23.3 %copy-start.2 = (s32[16,128]{1,0:T(8,128)S(1)}, s32[16,128]{1,0:T(8,128)}, u32[]{:S(2)}) copy-start(s32[16,128]{1,0:T(8,128)} %get-tuple-element.25.ids_ref) | copy-start | bytes 24580
  3.7 23.3 %copy-start.3 = (s32[1,128]{1,0:T(1,128)S(1)}, s32[1,128]{1,0:T(1,128)}, u32[]{:S(2)}) copy-start(s32[1,128]{1,0:T(1,128)} %get-tuple-element.26.row_ref) | copy-start | bytes 1540
  3.7 29.4 %slice-start = ((s8[4587520]{0:T(1024)(128)(4,1)}), s8[393216]{0:T(1024)(128)(4,1)S(1)}, s32[]{:S(2)}) async-start(s8[4587520]{0:T(1024)(128)(4,1)} %bitcast.17), calls=%async_computation.2 | async-start | bytes 786432
  3.7 23.3 %all-to-all-start = ((bf16[8,40,2048]{2,1,0:T(8,128)(2,1)}), bf16[8,40,2048]{2,1,0:T(8,128)(2,1)S(1)}, u32[]{:S(2)}, u32[]{:S(2)}) async-start(bf16[8,40,2048]{2,1,0:T(8,128)(2,1)} %get-tuple-element.27), calls=%async_computation | async-start | bytes 2621440 | tf_op jit(solution)/shard_map/all_to_all | solution.py:309
  27.0 6.1 %slice-start.1 = ((s8[4587520]{0:T(1024)(128)(4,1)}), s8[4194304]{0:T(1024)(128)(4,1)S(1)}, s32[]{:S(2)}) async-start(s8[4587520]{0:T(1024)(128)(4,1)} %bitcast.17), calls=%async_computation.3 | async-start | bytes 8388608
  27.0 23.9 %slice-start.2 = ((s8[4587520]{0:T(1024)(128)(4,1)}), s8[393216]{0:T(1024)(128)(4,1)S(1)}, s32[]{:S(2)}) async-start(s8[4587520]{0:T(1024)(128)(4,1)} %bitcast.23), calls=%async_computation.4 | async-start | bytes 786432
  33.1 2.3 %copy-start = (bf16[1,1,8,40,7168]{4,3,2,1,0:T(8,128)(2,1)S(1)}, bf16[1,1,8,40,7168]{4,3,2,1,0:T(8,128)(2,1)}, u32[]{:S(2)}) copy-start(bf16[1,1,8,40,7168]{4,3,2,1,0:T(8,128)(2,1)} %param.12) | copy-start | bytes 13762564
  35.4 15.5 %slice-start.3 = ((s8[4587520]{0:T(1024)(128)(4,1)}), s8[4194304]{0:T(1024)(128)(4,1)S(1)}, s32[]{:S(2)}) async-start(s8[4587520]{0:T(1024)(128)(4,1)} %bitcast.23), calls=%async_computation.5 | async-start | bytes 8388608
  41.0 36.6 %collective-permute-start.3 = (bf16[4,1040,128]{2,1,0:T(8,128)(2,1)S(1)}, bf16[4,1040,128]{2,1,0:T(8,128)(2,1)S(1)}, u32[]{:S(2)}, u32[]{:S(2)}) collective-permute-start(bf16[4,1040,128]{2,1,0:T(8,128)(2,1)S(1)} %get-tuple-element.32), channel_id=1, source_target_pairs={{0,1},{1,2},{2,3},{3,0},{4,5},{5,6},{6,7},{7,4},{8,9},{9,10},{10,1... | collective-permute-start | bytes 3194888 | tf_op jit(solution)/shard_map/ppermute | solution.py:317
  42.6 48.7 %collective-permute-start.4 = (bf16[4,1040,128]{2,1,0:T(8,128)(2,1)S(1)}, bf16[4,1040,128]{2,1,0:T(8,128)(2,1)S(1)}, u32[]{:S(2)}, u32[]{:S(2)}) collective-permute-start(bf16[4,1040,128]{2,1,0:T(8,128)(2,1)S(1)} %get-tuple-element.33), channel_id=1, source_target_pairs={{0,2},{1,3},{2,0},{3,1},{4,6},{5,7},{6,4},{7,5},{8,10},{9,11},{10,... | collective-permute-start | bytes 3194888 | tf_op jit(solution)/shard_map/ppermute | solution.py:317
  45.5 49.7 %collective-permute-start.5 = (bf16[4,1040,128]{2,1,0:T(8,128)(2,1)S(1)}, bf16[4,1040,128]{2,1,0:T(8,128)(2,1)S(1)}, u32[]{:S(2)}, u32[]{:S(2)}) collective-permute-start(bf16[4,1040,128]{2,1,0:T(8,128)(2,1)S(1)} %get-tuple-element.34), channel_id=1, source_target_pairs={{0,3},{1,0},{2,1},{3,2},{4,7},{5,4},{6,5},{7,6},{8,11},{9,8},{10,9... | collective-permute-start | bytes 3194888 | tf_op jit(solution)/shard_map/ppermute | solution.py:317
  46.9 54.4 %collective-permute-start.10 = (bf16[4,1040,128]{2,1,0:T(8,128)(2,1)S(1)}, bf16[4,1040,128]{2,1,0:T(8,128)(2,1)S(1)}, u32[]{:S(2)}, u32[]{:S(2)}) collective-permute-start(bf16[4,1040,128]{2,1,0:T(8,128)(2,1)S(1)} %get-tuple-element.43), channel_id=1, source_target_pairs={{0,12},{1,13},{2,14},{3,15},{4,0},{5,1},{6,2},{7,3},{8,4},{9,5},{1... | collective-permute-start | bytes 3194888 | tf_op jit(solution)/shard_map/ppermute | solution.py:320
  50.9 50.4 %collective-permute-start.11 = (bf16[4,1040,128]{2,1,0:T(8,128)(2,1)S(1)}, bf16[4,1040,128]{2,1,0:T(8,128)(2,1)S(1)}, u32[]{:S(2)}, u32[]{:S(2)}) collective-permute-start(bf16[4,1040,128]{2,1,0:T(8,128)(2,1)S(1)} %get-tuple-element.44), channel_id=1, source_target_pairs={{0,8},{1,9},{2,10},{3,11},{4,12},{5,13},{6,14},{7,15},{8,0},{9,1},... | collective-permute-start | bytes 3194888 | tf_op jit(solution)/shard_map/ppermute | solution.py:320
  77.6 49.4 %collective-permute-start = (bf16[1,1040,128]{2,1,0:T(8,128)(2,1)S(1)}, bf16[1,1040,128]{2,1,0:T(8,128)(2,1)S(1)}, u32[]{:S(2)}, u32[]{:S(2)}) collective-permute-start(bf16[1,1040,128]{2,1,0:T(8,128)(2,1)S(1)} %get-tuple-element.29), channel_id=1, source_target_pairs={{0,4},{1,5},{2,6},{3,7},{4,8},{5,9},{6,10},{7,11},{8,12},{9,13},{1... | collective-permute-start | bytes 798728 | tf_op jit(solution)/shard_map/ppermute | solution.py:320
  91.3 37.8 %collective-permute-start.1 = (bf16[1,1040,128]{2,1,0:T(8,128)(2,1)S(1)}, bf16[1,1040,128]{2,1,0:T(8,128)(2,1)S(1)}, u32[]{:S(2)}, u32[]{:S(2)}) collective-permute-start(bf16[1,1040,128]{2,1,0:T(8,128)(2,1)S(1)} %get-tuple-element.30), channel_id=1, source_target_pairs={{0,8},{1,9},{2,10},{3,11},{4,12},{5,13},{6,14},{7,15},{8,0},{9,1},... | collective-permute-start | bytes 798728 | tf_op jit(solution)/shard_map/ppermute | solution.py:320
  95.2 33.9 %collective-permute-start.2 = (bf16[1,1040,128]{2,1,0:T(8,128)(2,1)S(1)}, bf16[1,1040,128]{2,1,0:T(8,128)(2,1)S(1)}, u32[]{:S(2)}, u32[]{:S(2)}) collective-permute-start(bf16[1,1040,128]{2,1,0:T(8,128)(2,1)S(1)} %get-tuple-element.31), channel_id=1, source_target_pairs={{0,12},{1,13},{2,14},{3,15},{4,0},{5,1},{6,2},{7,3},{8,4},{9,5},{1... | collective-permute-start | bytes 798728 | tf_op jit(solution)/shard_map/ppermute | solution.py:320
  101.3 22.0 %collective-permute-start.9 = (bf16[4,1040,128]{2,1,0:T(8,128)(2,1)S(1)}, bf16[4,1040,128]{2,1,0:T(8,128)(2,1)S(1)}, u32[]{:S(2)}, u32[]{:S(2)}) collective-permute-start(bf16[4,1040,128]{2,1,0:T(8,128)(2,1)S(1)} %get-tuple-element.42), channel_id=1, source_target_pairs={{0,4},{1,5},{2,6},{3,7},{4,8},{5,9},{6,10},{7,11},{8,12},{9,13},{1... | collective-permute-start | bytes 3194888 | tf_op jit(solution)/shard_map/ppermute | solution.py:320
  101.3 30.8 %collective-permute-start.6 = (bf16[1,1040,128]{2,1,0:T(8,128)(2,1)S(1)}, bf16[1,1040,128]{2,1,0:T(8,128)(2,1)S(1)}, u32[]{:S(2)}, u32[]{:S(2)}) collective-permute-start(bf16[1,1040,128]{2,1,0:T(8,128)(2,1)S(1)} %get-tuple-element.39), channel_id=1, source_target_pairs={{0,1},{1,2},{2,3},{3,0},{4,5},{5,6},{6,7},{7,4},{8,9},{9,10},{10,1... | collective-permute-start | bytes 798728 | tf_op jit(solution)/shard_map/ppermute | solution.py:317
  123.3 10.3 %collective-permute-start.7 = (bf16[1,1040,128]{2,1,0:T(8,128)(2,1)S(1)}, bf16[1,1040,128]{2,1,0:T(8,128)(2,1)S(1)}, u32[]{:S(2)}, u32[]{:S(2)}) collective-permute-start(bf16[1,1040,128]{2,1,0:T(8,128)(2,1)S(1)} %get-tuple-element.40), channel_id=1, source_target_pairs={{0,2},{1,3},{2,0},{3,1},{4,6},{5,7},{6,4},{7,5},{8,10},{9,11},{10,... | collective-permute-start | bytes 798728 | tf_op jit(solution)/shard_map/ppermute | solution.py:317
  127.0 20.0 %collective-permute-start.12 = (bf16[3,1040,128]{2,1,0:T(8,128)(2,1)S(1)}, bf16[3,1040,128]{2,1,0:T(8,128)(2,1)S(1)}, u32[]{:S(2)}, u32[]{:S(2)}) collective-permute-start(bf16[3,1040,128]{2,1,0:T(8,128)(2,1)S(1)} %pad_maximum_fusion), channel_id=1, source_target_pairs={{0,4},{1,5},{2,6},{3,7},{4,8},{5,9},{6,10},{7,11},{8,12},{9,13},{1... | collective-permute-start | bytes 2396168 | tf_op jit(solution)/shard_map/ppermute | solution.py:320
  128.9 18.2 %copy-start.4 = (f32[1,7168,128]{2,1,0:T(8,128)S(1)}, f32[1,7168,128]{2,1,0:T(8,128)}, u32[]{:S(2)}) copy-start(f32[1,7168,128]{2,1,0:T(8,128)} %param.15) | copy-start | bytes 11010052
  129.0 11.2 %collective-permute-start.8 = (bf16[1,1040,128]{2,1,0:T(8,128)(2,1)S(1)}, bf16[1,1040,128]{2,1,0:T(8,128)(2,1)S(1)}, u32[]{:S(2)}, u32[]{:S(2)}) collective-permute-start(bf16[1,1040,128]{2,1,0:T(8,128)(2,1)S(1)} %get-tuple-element.41), channel_id=1, source_target_pairs={{0,3},{1,0},{2,1},{3,2},{4,7},{5,4},{6,5},{7,6},{8,11},{9,8},{10,9... | collective-permute-start | bytes 798728 | tf_op jit(solution)/shard_map/ppermute | solution.py:317
  129.1 20.9 %collective-permute-start.13 = (bf16[3,1040,128]{2,1,0:T(8,128)(2,1)S(1)}, bf16[3,1040,128]{2,1,0:T(8,128)(2,1)S(1)}, u32[]{:S(2)}, u32[]{:S(2)}) collective-permute-start(bf16[3,1040,128]{2,1,0:T(8,128)(2,1)S(1)} %pad_maximum_fusion.1), channel_id=1, source_target_pairs={{0,12},{1,13},{2,14},{3,15},{4,0},{5,1},{6,2},{7,3},{8,4},{9,5},{1... | collective-permute-start | bytes 2396168 | tf_op jit(solution)/shard_map/ppermute | solution.py:320
  132.1 20.2 %collective-permute-start.14 = (bf16[3,1040,128]{2,1,0:T(8,128)(2,1)S(1)}, bf16[3,1040,128]{2,1,0:T(8,128)(2,1)S(1)}, u32[]{:S(2)}, u32[]{:S(2)}) collective-permute-start(bf16[3,1040,128]{2,1,0:T(8,128)(2,1)S(1)} %pad_maximum_fusion.2), channel_id=1, source_target_pairs={{0,1},{1,2},{2,3},{3,0},{4,5},{5,6},{6,7},{7,4},{8,9},{9,10},{10,1... | collective-permute-start | bytes 2396168 | tf_op jit(solution)/shard_map/ppermute | solution.py:317
  133.5 23.8 %collective-permute-start.15 = (bf16[3,1040,128]{2,1,0:T(8,128)(2,1)S(1)}, bf16[3,1040,128]{2,1,0:T(8,128)(2,1)S(1)}, u32[]{:S(2)}, u32[]{:S(2)}) collective-permute-start(bf16[3,1040,128]{2,1,0:T(8,128)(2,1)S(1)} %pad_maximum_fusion.3), channel_id=1, source_target_pairs={{0,3},{1,0},{2,1},{3,2},{4,7},{5,4},{6,5},{7,6},{8,11},{9,8},{10,9... | collective-permute-start | bytes 2396168 | tf_op jit(solution)/shard_map/ppermute | solution.py:317
  140.2 22.6 %collective-permute-start.16 = (bf16[3,1040,128]{2,1,0:T(8,128)(2,1)S(1)}, bf16[3,1040,128]{2,1,0:T(8,128)(2,1)S(1)}, u32[]{:S(2)}, u32[]{:S(2)}) collective-permute-start(bf16[3,1040,128]{2,1,0:T(8,128)(2,1)S(1)} %pad_maximum_fusion.4), channel_id=1, source_target_pairs={{0,8},{1,9},{2,10},{3,11},{4,12},{5,13},{6,14},{7,15},{8,0},{9,1},... | collective-permute-start | bytes 2396168 | tf_op jit(solution)/shard_map/ppermute | solution.py:320
  147.0 18.4 %collective-permute-start.17 = (bf16[3,1040,128]{2,1,0:T(8,128)(2,1)S(1)}, bf16[3,1040,128]{2,1,0:T(8,128)(2,1)S(1)}, u32[]{:S(2)}, u32[]{:S(2)}) collective-permute-start(bf16[3,1040,128]{2,1,0:T(8,128)(2,1)S(1)} %pad_maximum_fusion.5), channel_id=1, source_target_pairs={{0,2},{1,3},{2,0},{3,1},{4,6},{5,7},{6,4},{7,5},{8,10},{9,11},{10,... | collective-permute-start | bytes 2396168 | tf_op jit(solution)/shard_map/ppermute | solution.py:317
  168.8 23.4 %all-to-all-start.1 = ((f32[16,1,128]{2,1,0:T(1,128)}), f32[16,1,128]{2,1,0:T(1,128)S(1)}, u32[]{:S(2)}, u32[]{:S(2)}) async-start(f32[16,1,128]{2,1,0:T(1,128)} %bitcast.12), calls=%async_computation.1 | async-start | bytes 16384 | tf_op jit(solution)/shard_map/all_to_all | solution.py:361

commit v3 on v2

--- a/solution.py
+++ b/solution.py
@@ -21,7 +21,10 @@
 TAIL = 16
 HALF = 8
 ORDER = (1, 3, 2)
-PRODUCTS_LIMITS = (44 * 1024 * 1024, 30 * 1024 * 1024)
+HOPS = (4, 5, 2, 6, 3, 7, 1)
+PLAN_LIMIT = 58 * 1024 * 1024
+FETCH_LIMIT = 16 * 1024 * 1024
+PRODUCTS_LIMIT = 16 * 1024 * 1024
 LIMIT = 20 * 1024 * 1024
 UPDATE_LIMIT = 20 * 1024 * 1024
 
@@ -32,12 +35,15 @@
 CONTRACT_LANES = (((1,), (1,)), ((), ()))
 
 
-def plan_kernel(routes_ref, gates_ref, cotan_ref, trigger_ref, table_ref, ids_ref, ids_row_ref, trig_scr):
+def plan_kernel(routes_ref, gates_ref, cotan_ref, trigger_ref, *refs):
+    table_refs, (ids_ref, ids_row_ref, trig_scr) = refs[:-3], refs[-3:]
     tokens = cotan_ref.shape[0]
-    experts = table_ref.shape[0]
+    experts = len(table_refs)
+    here = lax.axis_index("expert")
     routes = routes_ref[...]
     gates = gates_ref[...]
-    expert_ids = lax.broadcasted_iota(jnp.int32, (experts, tokens), 0)
+    rows = lax.broadcasted_iota(jnp.int32, (experts, tokens), 0)
+    expert_ids = (here // 2 * 2 + rows // 2 * 2) % experts + (here + rows) % 2
     first = routes[0:1, :] == expert_ids
     second = routes[1:2, :] == expert_ids
     named = jnp.where(first | second, 1.0, 0.0)
@@ -54,8 +60,8 @@
     for e in range(experts):
         pick = jnp.where((slot_ids == ranks[e : e + 1, :]) & (named[e : e + 1, :] > 0.5), 1.0, 0.0)
         gate_slot = jnp.sum(pick * gate_of[e : e + 1, :], axis=1, keepdims=True)
-        rows = jnp.dot(pick.astype(jnp.bfloat16), cotan, preferred_element_type=jnp.float32)
-        table_ref[e] = (rows * gate_slot).astype(jnp.bfloat16)
+        picked = jnp.dot(pick.astype(jnp.bfloat16), cotan, preferred_element_type=jnp.float32)
+        table_refs[e][...] = (picked * gate_slot).astype(jnp.bfloat16)
 
     trig_scr[...] = jnp.zeros_like(trig_scr)
     trig_scr[0:1, 0:BLOCKS] = trigger_ref[...].astype(jnp.float32)
@@ -81,11 +87,12 @@
     return pl.pallas_call(
         plan_kernel,
         out_shape=(
-            jax.ShapeDtypeStruct((experts, CAP, DW), jnp.bfloat16),
+            *[jax.ShapeDtypeStruct((CAP, DW), jnp.bfloat16)] * experts,
             jax.ShapeDtypeStruct((TRIG, LANES), jnp.int32),
             jax.ShapeDtypeStruct((1, LANES), jnp.int32),
         ),
         scratch_shapes=[pltpu.VMEM((8, LANES), jnp.float32)],
+        compiler_params=pltpu.CompilerParams(vmem_limit_bytes=PLAN_LIMIT),
         cost_estimate=pl.CostEstimate(flops=200_000_000, bytes_accessed=2_000_000, transcendentals=0),
         name="plan",
     )(routes, gates, cotan, trigger)
@@ -97,42 +104,88 @@
     left_ref[rows:, at] = prev
 
 
-def join_right(right_ref, slots_ref, cotan_ref):
-    rows = slots_ref.shape[0]
-    right_ref[0:rows, :] = slots_ref[...]
-    right_ref[rows:, :] = -cotan_ref[...]
-
-
-def products_kernel(start, count, z_first, ids_ref, place_ref, row_ref, now_hbm, prev_hbm, slots_ref, cotan_ref, *refs):
-    own_refs, far_refs = refs[0:SIDE], (None, *refs[SIDE : 2 * SIDE - 1])
-    left_ref, right_ref, now_sems, prev_sems = refs[2 * SIDE - 1 :]
-    rows = slots_ref.shape[0]
+def seen_from_here():
+    here = lax.axis_index("dp")
+    for t in range(SIDE):
+        for s in range(SIDE):
+            server = (here // SIDE + t) % SIDE * SIDE + (here + s) % SIDE
+            at = t * SIDE + s
+            yield pl.ds(pl.multiple_of(server * LANES, LANES), LANES), slice(at * LANES, (at + 1) * LANES)
+
+
+def fetch_kernel(ids_ref, now_hbm, prev_hbm, cotan_ref, right_ref, *refs):
+    left_refs, (now_sems, prev_sems) = refs[:-2], refs[-2:]
+    rows = cotan_ref.shape[0]
     copies = []
-    for j in range(count):
-        block = lax.rem(ids_ref[start + j, 0], 64)
+    for j in range(TRIG):
+        block = lax.rem(ids_ref[j, 0], 64)
         come = pl.ds(pl.multiple_of(block * BLOCK, BLOCK), BLOCK)
-        at = pl.ds(j * BLOCK, BLOCK)
+        left_ref, at = left_refs[j // HALF], pl.ds(j % HALF * BLOCK, BLOCK)
         copies.append(pltpu.make_async_copy(now_hbm.at[:, come], left_ref.at[pl.ds(0, rows), at], now_sems.at[j]))
         copies.append(pltpu.make_async_copy(prev_hbm.at[:, come], left_ref.at[pl.ds(rows, rows), at], prev_sems.at[j]))
     for copy in copies:
         copy.start()
-    for t in range(SIDE):
-        for s in range(SIDE):
-            server = ((place_ref[0] + t) % SIDE) * SIDE + (place_ref[1] + s) % SIDE
-            come = pl.ds(pl.multiple_of(server * LANES, LANES), LANES)
-            at = slice((t * SIDE + s) * LANES, (t * SIDE + s + 1) * LANES)
-            right_ref[0:rows, at] = slots_ref[:, come]
-            right_ref[rows:, at] = -cotan_ref[:, come]
+    for come, at in seen_from_here():
+        right_ref[:, at] = -cotan_ref[:, come]
+    for copy in copies:
+        copy.wait()
+
+
+def fetch(ids, now, prev, cotan):
+    rows = now.shape[0]
+    vmem = pl.BlockSpec(memory_space=pltpu.VMEM)
+    hbm = pl.BlockSpec(memory_space=pltpu.HBM)
+    left = jax.ShapeDtypeStruct((2 * rows, HALF * BLOCK), now.dtype)
+    return pl.pallas_call(
+        fetch_kernel,
+        out_shape=[jax.ShapeDtypeStruct(cotan.shape, cotan.dtype)] + [left] * (TRIG // HALF),
+        in_specs=[pl.BlockSpec(memory_space=pltpu.SMEM), hbm, hbm, vmem],
+        out_specs=[vmem] * (1 + TRIG // HALF),
+        scratch_shapes=[pltpu.SemaphoreType.DMA((TRIG,)), pltpu.SemaphoreType.DMA((TRIG,))],
+        compiler_params=pltpu.CompilerParams(vmem_limit_bytes=FETCH_LIMIT),
+        cost_estimate=pl.CostEstimate(flops=100_000_000, bytes_accessed=6_600_000, transcendentals=0),
+        name="fetch",
+    )(ids, now, prev, cotan)
+
+
+def arrange_kernel(*refs):
+    got_refs, (before_ref, out_ref) = refs[:-2], refs[-2:]
+    experts = len(got_refs)
+    slots = got_refs[0].shape[0]
+    here = lax.axis_index("expert")
+    for r, got_ref in enumerate(got_refs):
+        source = (here // 2 * 2 + experts - r // 2 * 2) % experts + (here + r) % 2
+        rows = pl.ds(pl.multiple_of(source * slots, 8), slots)
+        for come, at in seen_from_here():
+            out_ref[rows, at] = got_ref[:, come]
+    out_ref[experts * slots :, :] = before_ref[...]
+
+
+def arrange(got, before):
+    rows = len(got) * got[0].shape[0] + before.shape[0]
+    vmem = pl.BlockSpec(memory_space=pltpu.VMEM)
+    return pl.pallas_call(
+        arrange_kernel,
+        out_shape=jax.ShapeDtypeStruct((rows, before.shape[1]), before.dtype),
+        in_specs=[vmem] * (len(got) + 1),
+        out_specs=vmem,
+        compiler_params=pltpu.CompilerParams(vmem_limit_bytes=FETCH_LIMIT),
+        cost_estimate=pl.CostEstimate(flops=100_000_000, bytes_accessed=5_200_000, transcendentals=0),
+        name="arrange",
+    )(*got, before)
+
+
+def products_kernel(z_first, row_ref, left_ref, right_ref, *refs):
+    own_refs, far_refs = refs[0:SIDE], (None, *refs[SIDE:])
+    blocks = left_ref.shape[1]
     row = jnp.broadcast_to(row_ref[...].astype(jnp.float32), (TAIL, LANES)).astype(jnp.bfloat16)
-    behind = slice(count * BLOCK, count * BLOCK + TAIL)
+    behind = slice(blocks, blocks + TAIL)
     for k in range(SIDE):
         own_refs[k][0, behind, :] = row
         for m in range(1, SIDE):
             far_refs[m][k, behind, :] = row
-    for g in range(count // GROUP):
-        for copy in copies[2 * g * GROUP : 2 * (g + 1) * GROUP]:
-            copy.wait()
-        at = slice(g * GROUP * BLOCK, (g + 1) * GROUP * BLOCK)
+    for g in range(0, blocks, GROUP * BLOCK):
+        at = slice(g, g + GROUP * BLOCK)
         for t in range(SIDE):
             acc = lax.dot_general(
                 left_ref[:, at],
@@ -149,36 +202,24 @@
                     far_refs[first][second, at, :] = piece
 
 
-def products(ids, place, row, now, prev, slots, cotan, start, count, z_first):
-    rows = now.shape[0]
+def products(row, left, right, z_first):
+    blocks = left.shape[1]
     vmem = pl.BlockSpec(memory_space=pltpu.VMEM)
-    smem = pl.BlockSpec(memory_space=pltpu.SMEM)
-    hbm = pl.BlockSpec(memory_space=pltpu.HBM)
-    return pl.pallas_call(
-        functools.partial(products_kernel, start, count, z_first),
-        out_shape=[jax.ShapeDtypeStruct((1, count * BLOCK + TAIL, LANES), jnp.bfloat16)] * SIDE
-        + [jax.ShapeDtypeStruct((SIDE, count * BLOCK + TAIL, LANES), jnp.bfloat16)] * (SIDE - 1),
-        in_specs=[smem, smem, vmem, hbm, hbm, vmem, vmem],
+    return pl.pallas_call(
+        functools.partial(products_kernel, z_first),
+        out_shape=[jax.ShapeDtypeStruct((1, blocks + TAIL, LANES), jnp.bfloat16)] * SIDE
+        + [jax.ShapeDtypeStruct((SIDE, blocks + TAIL, LANES), jnp.bfloat16)] * (SIDE - 1),
+        in_specs=[vmem] * 3,
         out_specs=[vmem] * (2 * SIDE - 1),
-        scratch_shapes=[
-            pltpu.VMEM((2 * rows, count * BLOCK), jnp.bfloat16),
-            pltpu.VMEM((2 * rows, DW), jnp.bfloat16),
-            pltpu.SemaphoreType.DMA((count,)),
-            pltpu.SemaphoreType.DMA((count,)),
-        ],
-        compiler_params=pltpu.CompilerParams(vmem_limit_bytes=PRODUCTS_LIMITS[z_first]),
+        compiler_params=pltpu.CompilerParams(vmem_limit_bytes=PRODUCTS_LIMIT),
         cost_estimate=pl.CostEstimate(
-            flops=4 * rows * BLOCK * DW * count, bytes_accessed=count * 700_000 + 2_600_000, transcendentals=0
+            flops=2 * left.shape[0] * blocks * DW, bytes_accessed=8_000_000, transcendentals=0
         ),
         name="products",
-    )(ids, place, row, now, prev, slots, cotan)
-
-
-def norms_kernel(now_ref, prev_ref, slots_ref, cotan_ref, out_ref, left_ref, right_ref):
-    @pl.when(pl.program_id(0) == 0)
-    def _():
-        join_right(right_ref, slots_ref, cotan_ref)
-
+    )(row, left, right)
+
+
+def norms_kernel(now_ref, prev_ref, right_ref, out_ref, left_ref):
     join(left_ref, slice(None), now_ref[...], prev_ref[...])
     totals = [jnp.zeros((1, LANES), jnp.float32)] * GROUP
     for n in range(DW // WIDE):
@@ -197,7 +238,7 @@
         out_ref[j] = totals[j]
 
 
-def norms(now, prev, slots, cotan):
+def norms(now, prev, right):
     rows = now.shape[0]
     return pl.pallas_call(
         norms_kernel,
@@ -206,20 +247,18 @@
         in_specs=[
             pl.BlockSpec((rows, GROUP * BLOCK), lambda b: (0, b)),
             pl.BlockSpec((rows, GROUP * BLOCK), lambda b: (0, b)),
-            pl.BlockSpec((rows, DW), lambda b: (0, 0)),
-            pl.BlockSpec((rows, DW), lambda b: (0, 0)),
+            pl.BlockSpec((2 * rows, DW), lambda b: (0, 0)),
         ],
         out_specs=pl.BlockSpec((GROUP, 1, LANES), lambda b: (b, 0, 0)),
         scratch_shapes=[
             pltpu.VMEM((2 * rows, GROUP * BLOCK), jnp.bfloat16),
-            pltpu.VMEM((2 * rows, DW), jnp.bfloat16),
         ],
         compiler_params=pltpu.CompilerParams(dimension_semantics=("arbitrary",), vmem_limit_bytes=LIMIT),
         cost_estimate=pl.CostEstimate(
             flops=4 * rows * FFW * DW, bytes_accessed=4 * rows * FFW + 2_600_000, transcendentals=0
         ),
         name="norms",
-    )(now, prev, slots, cotan)
+    )(now, prev, right)
 
 
 def update_kernel(pieces, last, base_ref, *refs):
@@ -293,6 +332,10 @@
     )(base, *got)
 
 
+def cross(experts, r):
+    return [(e, (e // 2 * 2 + r // 2 * 2) % experts + (e + r) % 2) for e in range(experts)]
+
+
 def shift(workers, dz, dy):
     side = SIDE
     return [
@@ -304,14 +347,15 @@
     experts = lax.axis_size("expert")
     workers = lax.axis_size("dp")
     columns = DW // workers
-    table, ids, ids_row = plan(routes.T, gate_probs.T, cotangents, trigger.reshape(1, BLOCKS), experts)
+    *tables, ids, ids_row = plan(routes.T, gate_probs.T, cotangents, trigger.reshape(1, BLOCKS), experts)
     exchange = functools.partial(lax.all_to_all, split_axis=0, concat_axis=0, tiled=True)
-    slots = exchange(table, "expert").reshape(-1, DW)
+    arrived = [tables[0]] + [None] * (experts - 1)
+    for r in HOPS:
+        arrived[r] = lax.ppermute(tables[r], "expert", cross(experts, r))
     now = hidden_now.reshape(-1, FFW)
     prev = hidden_prev.reshape(-1, FFW)
-    cotan = cotan_prev.reshape(-1, DW)
-    here = lax.axis_index("dp")
-    place = jnp.stack([here // SIDE, here % SIDE]).astype(jnp.int32)
+    before, left_a, left_b = fetch(ids, now, prev, cotan_prev.reshape(-1, DW))
+    right = arrange(arrived, before)
 
     def along_y(x, k):
         return lax.ppermute(x, "dp", shift(workers, 0, k))
@@ -319,8 +363,8 @@
     def along_z(x, k):
         return lax.ppermute(x, "dp", shift(workers, k, 0))
 
-    def stage_one(start, z_first, near, far):
-        sent = products(ids, place, ids_row, now, prev, slots, cotan, start, HALF, z_first)
+    def stage_one(left, z_first, near, far):
+        sent = products(ids_row, left, right, z_first)
         own, relay = {0: sent[0]}, {}
         for k in ORDER:
             relay[k] = near(sent[SIDE - 1 + k], k)
@@ -334,9 +378,9 @@
             got[k] = far(jnp.stack([relay[j][k] for j in range(1, SIDE)]), k)
         return got
 
-    own_a, relay_a = stage_one(0, False, along_y, along_z)
-    own_b, relay_b = stage_one(HALF, True, along_z, along_y)
-    squared = norms(now, prev, slots, cotan)
+    own_a, relay_a = stage_one(left_a, False, along_y, along_z)
+    own_b, relay_b = stage_one(left_b, True, along_z, along_y)
+    squared = norms(now, prev, right)
     relay_a, squared = lax.optimization_barrier((relay_a, squared))
     second_a = stage_two(relay_a, along_z)
     second_b = stage_two(relay_b, along_y)

time: 193 us -> 183 us (0.948)
  starting transfers between devices: 52.1 us -> 39.3 us
  local copies, waits for them, and re-layouts: 2.66 us -> 6.97 us
  Pallas kernels: 50.1 us -> 48.1 us
    ppermute x9, waiting for transfers between devices: 33.5 us -> 54.3 us  [along_z(): return lax.ppermute(x, 'dp', shift(workers, k, 0))]
    all_to_all x1 -> x0, waiting for transfers between devices: 18.7 us -> none  [local(): slots = exchange(table, 'expert').reshape(-1, DW)]
    all_to_all x1, starting transfers between devices: 15.8 us -> 3.63 us  [local(): exchange(squares.reshape(workers, 1, LANES), 'dp').reshape(workers, LANES)]
    ppermute x0 -> x7, starting transfers between devices: none -> 8.19 us  [local(): arrived[r] = lax.ppermute(tables[r], 'expert', cross(experts, r))]
    all_to_all x1 -> x0, starting transfers between devices: 4.56 us -> none  [local(): slots = exchange(table, 'expert').reshape(-1, DW)]
    ppermute x9, waiting for transfers between devices: 26 us -> 21.6 us  [along_y(): return lax.ppermute(x, 'dp', shift(workers, 0, k))]
    unnamed x18 -> x22, local copies, waits for them, and re-layouts: 2.34 us -> 6.65 us
    ppermute x9, starting transfers between devices: 16.5 us -> 13.4 us  [along_y(): return lax.ppermute(x, 'dp', shift(workers, 0, k))]
  transfers between devices with their start and end apart: 20 -> 26, of which waited for: 12 -> 11; matrix products, arithmetic and copies ran while one was open for 1% -> 1% of each run, Pallas kernels for 17% -> 21%
where the time goes in v3:
time: 183 us
  waiting for transfers between devices  85.9 us (47%)
  Pallas kernels  48.1 us (26%)
  starting transfers between devices  39.3 us (21%)
  local copies, waits for them, and re-layouts  6.97 us (4%)
    ppermute x9, waiting for transfers between devices, along_z(): return lax.ppermute(x, 'dp', shift(workers, k, 0))  54.3 us
    pallas_call x1, Pallas kernels, norms(): pl.pallas_call(norms_kernel, out_shape=jax.ShapeDtypeStruct((BLOCKS, 1, L...  26.8 us
    ppermute x9, waiting for transfers between devices, along_y(): return lax.ppermute(x, 'dp', shift(workers, 0, k))  21.6 us
    ppermute x9, starting transfers between devices, along_z(): return lax.ppermute(x, 'dp', shift(workers, k, 0))  14.1 us
    ppermute x9, starting transfers between devices, along_y(): return lax.ppermute(x, 'dp', shift(workers, 0, k))  13.4 us
    pallas_call x3, Pallas kernels, update(): pl.pallas_call(functools.partial(update_kernel, pieces, last), out_shape=...  8.71 us
    ppermute x7, starting transfers between devices, local(): arrived[r] = lax.ppermute(tables[r], 'expert', cross(experts, r))  8.19 us
    all_to_all x1, waiting for transfers between devices, local(): exchange(squares.reshape(workers, 1, LANES), 'dp').reshape(workers, LANES)  7.08 us
  transfers between devices with their start and end apart: 26, of which 11 were waited for; matrix products, arithmetic and copies ran while one was open for 1% of the time, Pallas kernels for 21%

profile of v3, /device:TPU:0, one launch (start us, length us, event | category | flops | bytes accessed | tf_op | source)
XLA Modules:
  0.0 182.8 jit_solution(10171936558147852610)
XLA Ops:
  0.6 2.7 %plan.1 = (bf16[40,2048]{1,0:T(8,128)(2,1)}, bf16[40,2048]{1,0:T(8,128)(2,1)}, bf16[40,2048]{1,0:T(8,128)(2,1)}, bf16[40,2048]{1,0:T(8,128)(2,1)}, bf16[40,2048]...) custom-call(s32[2,128]{1,0:T(2,128)} %bitcast.23, ...), custom_call_target="tpu_custom_call" | custom-call | flops 200000000 | bytes 2000000 | tf_op jit(solution)/shard_map/plan/pallas_call | solution.py:87
  3.3 1.7 collective-permute-start.1
  6.2 1.6 collective-permute-start.3
  7.9 1.6 collective-permute-start.4
  9.5 1.7 collective-permute-start.5
  12.2 2.3 %copy-done = bf16[1,1,8,40,7168]{4,3,2,1,0:T(8,128)(2,1)S(1)} copy-done((bf16[1,1,8,40,7168]{4,3,2,1,0:T(8,128)(2,1)S(1)}, bf16[1,1,8,40,7168]{4,3,2,1,0:T(8,128)(2,1)}, u32[]{:S(2)}) %copy-start) | copy-done | bytes 4587544
  14.5 2.3 %copy-done.1 = bf16[1,1,8,40,7168]{4,3,2,1,0:T(8,128)(2,1)S(1)} copy-done((bf16[1,1,8,40,7168]{4,3,2,1,0:T(8,128)(2,1)S(1)}, bf16[1,1,8,40,7168]{4,3,2,1,0:T(8,128)(2,1)}, u32[]{:S(2)}) %copy-start.1) | copy-done | bytes 4587544
  16.8 1.3 copy-done.2
  18.8 2.3 %fetch.1 = (bf16[320,2048]{1,0:T(8,128)(2,1)S(1)}, bf16[640,1024]{1,0:T(8,128)(2,1)S(1)}, bf16[640,1024]{1,0:T(8,128)(2,1)S(1)}) custom-call(s32[16,128]{1,0:T(8,128)S(1)} %copy-done.4, bf16[320,7168]{1,0:T(8,128)(2,1)S(1)} %bitcast.13, bf16[320,7168]{1,0:T(8,128)(2,1)S(1)} %bitcast.17, bf16[320,2048]{1,0:T(8,128)(2,1)S(1)} %bitcast.21), custom_call_target="tpu_custom_call" | custom-call | flops 100000000 | bytes 6600000 | tf_op jit(solution)/shard_map/fetch/pallas_call | solution.py:139
  24.1 3.5 %products.2 = (bf16[1,1040,128]{2,1,0:T(8,128)(2,1)S(1)}, bf16[1,1040,128]{2,1,0:T(8,128)(2,1)S(1)}, bf16[1,1040,128]{2,1,0:T(8,128)(2,1)S(1)}, bf16[1,1040,128]...) custom-call(s32[1,128]{1,0:T(1,128)S(1)} %copy-done.6, ...), custom_call_target="tpu_custom_call" | custom-call | flops 2684354560 | bytes 8000000 | tf_op jit(solution)/shard_map/products/pallas_call | solution.py:208
  27.6 1.6 collective-permute-start.10
  29.3 2.9 %collective-permute-start.11 = (bf16[4,1040,128]{2,1,0:T(8,128)(2,1)S(1)}, bf16[4,1040,128]{2,1,0:T(8,128)(2,1)S(1)}, u32[]{:S(2)}, u32[]{:S(2)}) collective-permute-start(bf16[4,1040,128]{2,1,0:T(8,128)(2,1)S(1)} %get-tuple-element.52), channel_id=1, source_target_pairs={{0,2},{1,3},{2,0},{3,1},{4,6},{5,7},{6,4},{7,5},{8,10},{9,11},{10,... | collective-permute-start | bytes 3194888 | tf_op jit(solution)/shard_map/ppermute | solution.py:361
  32.2 1.3 collective-permute-start.12
  33.5 3.5 %products.3 = (bf16[1,1040,128]{2,1,0:T(8,128)(2,1)S(1)}, bf16[1,1040,128]{2,1,0:T(8,128)(2,1)S(1)}, bf16[1,1040,128]{2,1,0:T(8,128)(2,1)S(1)}, bf16[1,1040,128]...) custom-call(s32[1,128]{1,0:T(1,128)S(1)} %copy-done.6, ...), custom_call_target="tpu_custom_call" | custom-call | flops 2684354560 | bytes 8000000 | tf_op jit(solution)/shard_map/products/pallas_call | solution.py:208
  37.0 4.1 %collective-permute-start.17 = (bf16[4,1040,128]{2,1,0:T(8,128)(2,1)S(1)}, bf16[4,1040,128]{2,1,0:T(8,128)(2,1)S(1)}, u32[]{:S(2)}, u32[]{:S(2)}) collective-permute-start(bf16[4,1040,128]{2,1,0:T(8,128)(2,1)S(1)} %get-tuple-element.63), channel_id=1, source_target_pairs={{0,12},{1,13},{2,14},{3,15},{4,0},{5,1},{6,2},{7,3},{8,4},{9,5},{1... | collective-permute-start | bytes 3194888 | tf_op jit(solution)/shard_map/ppermute | solution.py:364
  41.3 26.8 %norms.1 = f32[56,1,128]{2,1,0:T(1,128)S(1)} custom-call(bf16[320,7168]{1,0:T(8,128)(2,1)S(1)} %bitcast.16, bf16[320,7168]{1,0:T(8,128)(2,1)S(1)} %bitcast.20, bf16[640,2048]{1,0:T(8,128)(2,1)S(1)} %arrange.1.right_ref), custom_call_target="tpu_custom_call" | custom-call | flops 18790481920 | bytes 11775040 | tf_op jit(solution)/shard_map/norms/pallas_call | solution.py:243
  69.3 9.5 %collective-permute-done.11.refs_6_ = bf16[4,1040,128]{2,1,0:T(8,128)(2,1)S(1)} collective-permute-done((bf16[4,1040,128]{2,1,0:T(8,128)(2,1)S(1)}, bf16[4,1040,128]{2,1,0:T(8,128)(2,1)S(1)}, u32[]{:S(2)}, u32[]{:S(2)}) %collective-permute-start.11) | collective-permute-done | bytes 1064992 | tf_op jit(solution)/shard_map/ppermute | solution.py:361
  78.8 3.9 %collective-permute-start.8 = (bf16[1,1040,128]{2,1,0:T(8,128)(2,1)S(1)}, bf16[1,1040,128]{2,1,0:T(8,128)(2,1)S(1)}, u32[]{:S(2)}, u32[]{:S(2)}) collective-permute-start(bf16[1,1040,128]{2,1,0:T(8,128)(2,1)S(1)} %get-tuple-element.49), channel_id=1, source_target_pairs={{0,8},{1,9},{2,10},{3,11},{4,12},{5,13},{6,14},{7,15},{8,0},{9,1},... | collective-permute-start | bytes 798728 | tf_op jit(solution)/shard_map/ppermute | solution.py:364
  83.5 10.1 %collective-permute-done.17.refs_12_ = bf16[4,1040,128]{2,1,0:T(8,128)(2,1)S(1)} collective-permute-done((bf16[4,1040,128]{2,1,0:T(8,128)(2,1)S(1)}, bf16[4,1040,128]{2,1,0:T(8,128)(2,1)S(1)}, u32[]{:S(2)}, u32[]{:S(2)}) %collective-permute-start.17) | collective-permute-done | bytes 1064992 | tf_op jit(solution)/shard_map/ppermute | solution.py:364
  94.5 23.5 %collective-permute-done.16.refs_11_ = bf16[4,1040,128]{2,1,0:T(8,128)(2,1)S(1)} collective-permute-done((bf16[4,1040,128]{2,1,0:T(8,128)(2,1)S(1)}, bf16[4,1040,128]{2,1,0:T(8,128)(2,1)S(1)}, u32[]{:S(2)}, u32[]{:S(2)}) %collective-permute-start.16) | collective-permute-done | bytes 1064992 | tf_op jit(solution)/shard_map/ppermute | solution.py:364
  119.5 2.6 %collective-permute-start.15 = (bf16[1,1040,128]{2,1,0:T(8,128)(2,1)S(1)}, bf16[1,1040,128]{2,1,0:T(8,128)(2,1)S(1)}, u32[]{:S(2)}, u32[]{:S(2)}) collective-permute-start(bf16[1,1040,128]{2,1,0:T(8,128)(2,1)S(1)} %get-tuple-element.61), channel_id=1, source_target_pairs={{0,3},{1,0},{2,1},{3,2},{4,7},{5,4},{6,5},{7,6},{8,11},{9,8},{10,9... | collective-permute-start | bytes 798728 | tf_op jit(solution)/shard_map/ppermute | solution.py:361
  122.0 3.2 %collective-permute-start.20 = (bf16[3,1040,128]{2,1,0:T(8,128)(2,1)S(1)}, bf16[3,1040,128]{2,1,0:T(8,128)(2,1)S(1)}, u32[]{:S(2)}, u32[]{:S(2)}) collective-permute-start(bf16[3,1040,128]{2,1,0:T(8,128)(2,1)S(1)} %pad_maximum_fusion.1), channel_id=1, source_target_pairs={{0,12},{1,13},{2,14},{3,15},{4,0},{5,1},{6,2},{7,3},{8,4},{9,5},{1... | collective-permute-start | bytes 2396168 | tf_op jit(solution)/shard_map/ppermute | solution.py:364
  125.3 3.2 %collective-permute-done.14.refs_9_ = bf16[1,1040,128]{2,1,0:T(8,128)(2,1)S(1)} collective-permute-done((bf16[1,1040,128]{2,1,0:T(8,128)(2,1)S(1)}, bf16[1,1040,128]{2,1,0:T(8,128)(2,1)S(1)}, u32[]{:S(2)}, u32[]{:S(2)}) %collective-permute-start.14) | collective-permute-done | bytes 266272 | tf_op jit(solution)/shard_map/ppermute | solution.py:361
  129.8 2.8 %collective-permute-done.15.refs_10_ = bf16[1,1040,128]{2,1,0:T(8,128)(2,1)S(1)} collective-permute-done((bf16[1,1040,128]{2,1,0:T(8,128)(2,1)S(1)}, bf16[1,1040,128]{2,1,0:T(8,128)(2,1)S(1)}, u32[]{:S(2)}, u32[]{:S(2)}) %collective-permute-start.15) | collective-permute-done | bytes 266272 | tf_op jit(solution)/shard_map/ppermute | solution.py:361
  133.4 20.7 %collective-permute-done.19.refs_0_ = bf16[3,1040,128]{2,1,0:T(8,128)(2,1)S(1)} collective-permute-done((bf16[3,1040,128]{2,1,0:T(8,128)(2,1)S(1)}, bf16[3,1040,128]{2,1,0:T(8,128)(2,1)S(1)}, u32[]{:S(2)}, u32[]{:S(2)}) %collective-permute-start.19) | collective-permute-done | bytes 798752 | tf_op jit(solution)/shard_map/ppermute | solution.py:364
  154.1 2.2 %collective-permute-start.24 = (bf16[3,1040,128]{2,1,0:T(8,128)(2,1)S(1)}, bf16[3,1040,128]{2,1,0:T(8,128)(2,1)S(1)}, u32[]{:S(2)}, u32[]{:S(2)}) collective-permute-start(bf16[3,1040,128]{2,1,0:T(8,128)(2,1)S(1)} %pad_maximum_fusion.5), channel_id=1, source_target_pairs={{0,2},{1,3},{2,0},{3,1},{4,6},{5,7},{6,4},{7,5},{8,10},{9,11},{10,... | collective-permute-start | bytes 2396168 | tf_op jit(solution)/shard_map/ppermute | solution.py:361
  156.2 2.9 %update.2.base_ref = f32[7168,128]{1,0:T(8,128)S(1)} custom-call(f32[7168,128]{1,0:T(8,128)S(1)} %bitcast.22, bf16[1,1040,128]{2,1,0:T(8,128)(2,1)S(1)} %get-tuple-element.47.refs_0_, bf16[1,1040,128]{2,1,0:T(8,128)(2,1)S(1)} %collective-permute-done.7.refs_1_, bf16[1,1040,128]{2,1,0:T(8,128)(2,1)S(1)} %collective-permute-done.8.refs_2_, ...), custom_call_target="tpu_custom_call" | custom-call | flops 5000000000 | bytes 16000000 | tf_op jit(solution)/shard_map/update/pallas_call | solution.py:318
  159.2 2.4 %update.3.base_ref = f32[7168,128]{1,0:T(8,128)S(1)} custom-call(f32[7168,128]{1,0:T(8,128)S(1)} %update.2.base_ref, bf16[3,1040,128]{2,1,0:T(8,128)(2,1)S(1)} %collective-permute-done.19.refs_0_, bf16[3,1040,128]{2,1,0:T(8,128)(2,1)S(1)} %collective-permute-done.20.refs_1_, bf16[3,1040,128]{2,1,0:T(8,128)(2,1)S(1)} %collective-permute-done.21.refs_2_, ...), custom_call_target="tpu_custom_call" | custom-call | flops 5000000000 | bytes 16000000 | tf_op jit(solution)/shard_map/update/pallas_call | solution.py:318
  161.7 6.0 %collective-permute-done.24.refs_1_ = bf16[3,1040,128]{2,1,0:T(8,128)(2,1)S(1)} collective-permute-done((bf16[3,1040,128]{2,1,0:T(8,128)(2,1)S(1)}, bf16[3,1040,128]{2,1,0:T(8,128)(2,1)S(1)}, u32[]{:S(2)}, u32[]{:S(2)}) %collective-permute-start.24) | collective-permute-done | bytes 798752 | tf_op jit(solution)/shard_map/ppermute | solution.py:361
  167.7 3.3 %update_last.1 = (f32[7168,128]{1,0:T(8,128)}, f32[16,128]{1,0:T(8,128)}) custom-call(f32[7168,128]{1,0:T(8,128)S(1)} %update.3.base_ref, bf16[3,1040,128]{2,1,0:T(8,128)(2,1)S(1)} %collective-permute-done.23.refs_0_, bf16[3,1040,128]{2,1,0:T(8,128)(2,1)S(1)} %collective-permute-done.24.refs_1_), custom_call_target="tpu_custom_call" | custom-call | flops 5000000000 | bytes 16000000 | tf_op jit(solution)/shard_map/update_last/pallas_call | solution.py:318
  171.0 3.6 %all-to-all-start = ((f32[16,1,128]{2,1,0:T(1,128)}), f32[16,1,128]{2,1,0:T(1,128)S(1)}, u32[]{:S(2)}, u32[]{:S(2)}) async-start(f32[16,1,128]{2,1,0:T(1,128)} %bitcast.9), calls=%async_computation | async-start | bytes 16384 | tf_op jit(solution)/shard_map/all_to_all | solution.py:405
  175.2 7.1 %all-to-all-done = f32[16,1,128]{2,1,0:T(1,128)S(1)} async-done(((f32[16,1,128]{2,1,0:T(1,128)}), f32[16,1,128]{2,1,0:T(1,128)S(1)}, u32[]{:S(2)}, u32[]{:S(2)}) %all-to-all-start) | async-done | bytes 8224 | tf_op jit(solution)/shard_map/all_to_all | solution.py:405
  (67 shorter events, 13.5 us)
Async XLA Ops:
  3.3 6.1 %collective-permute-start = (bf16[40,2048]{1,0:T(8,128)(2,1)}, bf16[40,2048]{1,0:T(8,128)(2,1)S(1)}, u32[]{:S(2)}, u32[]{:S(2)}) collective-permute-start(bf16[40,2048]{1,0:T(8,128)(2,1)} %get-tuple-element.39), channel_id=1, source_target_pairs={{0,16},{16,0},{32,48},{48,32},{64,80},{80,64},{96,112},{112,96},{1... | collective-permute-start | bytes 491528 | tf_op jit(solution)/shard_map/ppermute | solution.py:354
  3.3 8.6 %collective-permute-start.1 = (bf16[40,2048]{1,0:T(8,128)(2,1)}, bf16[40,2048]{1,0:T(8,128)(2,1)S(1)}, u32[]{:S(2)}, u32[]{:S(2)}) collective-permute-start(bf16[40,2048]{1,0:T(8,128)(2,1)} %get-tuple-element.40), channel_id=1, source_target_pairs={{0,32},{16,48},{32,64},{48,80},{64,96},{80,112},{96,0},{112,16},{1... | collective-permute-start | bytes 491528 | tf_op jit(solution)/shard_map/ppermute | solution.py:354
  5.0 16.2 %collective-permute-start.2 = (bf16[40,2048]{1,0:T(8,128)(2,1)}, bf16[40,2048]{1,0:T(8,128)(2,1)S(1)}, u32[]{:S(2)}, u32[]{:S(2)}) collective-permute-start(bf16[40,2048]{1,0:T(8,128)(2,1)} %get-tuple-element.41), channel_id=1, source_target_pairs={{0,48},{16,32},{32,80},{48,64},{64,112},{80,96},{96,16},{112,0},{1... | collective-permute-start | bytes 491528 | tf_op jit(solution)/shard_map/ppermute | solution.py:354
  6.2 14.9 %collective-permute-start.3 = (bf16[40,2048]{1,0:T(8,128)(2,1)}, bf16[40,2048]{1,0:T(8,128)(2,1)S(1)}, u32[]{:S(2)}, u32[]{:S(2)}) collective-permute-start(bf16[40,2048]{1,0:T(8,128)(2,1)} %get-tuple-element.42), channel_id=1, source_target_pairs={{0,64},{16,80},{32,96},{48,112},{64,0},{80,16},{96,32},{112,48},{1... | collective-permute-start | bytes 491528 | tf_op jit(solution)/shard_map/ppermute | solution.py:354
  7.9 14.6 %collective-permute-start.4 = (bf16[40,2048]{1,0:T(8,128)(2,1)}, bf16[40,2048]{1,0:T(8,128)(2,1)S(1)}, u32[]{:S(2)}, u32[]{:S(2)}) collective-permute-start(bf16[40,2048]{1,0:T(8,128)(2,1)} %get-tuple-element.43), channel_id=1, source_target_pairs={{0,80},{16,64},{32,112},{48,96},{64,16},{80,0},{96,48},{112,32},{1... | collective-permute-start | bytes 491528 | tf_op jit(solution)/shard_map/ppermute | solution.py:354
  9.5 13.0 %collective-permute-start.5 = (bf16[40,2048]{1,0:T(8,128)(2,1)}, bf16[40,2048]{1,0:T(8,128)(2,1)S(1)}, u32[]{:S(2)}, u32[]{:S(2)}) collective-permute-start(bf16[40,2048]{1,0:T(8,128)(2,1)} %get-tuple-element.44), channel_id=1, source_target_pairs={{0,96},{16,112},{32,0},{48,16},{64,32},{80,48},{96,64},{112,80},{1... | collective-permute-start | bytes 491528 | tf_op jit(solution)/shard_map/ppermute | solution.py:354
  11.9 11.6 %collective-permute-start.6 = (bf16[40,2048]{1,0:T(8,128)(2,1)}, bf16[40,2048]{1,0:T(8,128)(2,1)S(1)}, u32[]{:S(2)}, u32[]{:S(2)}) collective-permute-start(bf16[40,2048]{1,0:T(8,128)(2,1)} %get-tuple-element.45), channel_id=1, source_target_pairs={{0,112},{16,96},{32,16},{48,0},{64,48},{80,32},{96,80},{112,64},{1... | collective-permute-start | bytes 491528 | tf_op jit(solution)/shard_map/ppermute | solution.py:354
  18.8 4.7 %copy-start.3 = (bf16[40,2048]{1,0:T(8,128)(2,1)S(1)}, bf16[40,2048]{1,0:T(8,128)(2,1)}, u32[]{:S(2)}) copy-start(bf16[40,2048]{1,0:T(8,128)(2,1)} %get-tuple-element.38.refs_0_) | copy-start | bytes 491524
  24.1 17.1 %slice-start = ((s8[4587520]{0:T(1024)(128)(4,1)}), s8[4194304]{0:T(1024)(128)(4,1)S(1)}, s32[]{:S(2)}) async-start(s8[4587520]{0:T(1024)(128)(4,1)} %bitcast.14), calls=%async_computation.1 | async-start | bytes 8388608
  24.1 17.1 %slice-start.2 = ((s8[4587520]{0:T(1024)(128)(4,1)}), s8[4194304]{0:T(1024)(128)(4,1)S(1)}, s32[]{:S(2)}) async-start(s8[4587520]{0:T(1024)(128)(4,1)} %bitcast.18), calls=%async_computation.3 | async-start | bytes 8388608
  27.6 40.5 %collective-permute-start.10 = (bf16[4,1040,128]{2,1,0:T(8,128)(2,1)S(1)}, bf16[4,1040,128]{2,1,0:T(8,128)(2,1)S(1)}, u32[]{:S(2)}, u32[]{:S(2)}) collective-permute-start(bf16[4,1040,128]{2,1,0:T(8,128)(2,1)S(1)} %get-tuple-element.51), channel_id=1, source_target_pairs={{0,1},{1,2},{2,3},{3,0},{4,5},{5,6},{6,7},{7,4},{8,9},{9,10},{10,1... | collective-permute-start | bytes 3194888 | tf_op jit(solution)/shard_map/ppermute | solution.py:361
  29.3 49.5 %collective-permute-start.11 = (bf16[4,1040,128]{2,1,0:T(8,128)(2,1)S(1)}, bf16[4,1040,128]{2,1,0:T(8,128)(2,1)S(1)}, u32[]{:S(2)}, u32[]{:S(2)}) collective-permute-start(bf16[4,1040,128]{2,1,0:T(8,128)(2,1)S(1)} %get-tuple-element.52), channel_id=1, source_target_pairs={{0,2},{1,3},{2,0},{3,1},{4,6},{5,7},{6,4},{7,5},{8,10},{9,11},{10,... | collective-permute-start | bytes 3194888 | tf_op jit(solution)/shard_map/ppermute | solution.py:361
  32.2 9.1 %slice-start.1 = ((s8[4587520]{0:T(1024)(128)(4,1)}), s8[393216]{0:T(1024)(128)(4,1)S(1)}, s32[]{:S(2)}) async-start(s8[4587520]{0:T(1024)(128)(4,1)} %bitcast.14), calls=%async_computation.2 | async-start | bytes 786432
  32.2 9.1 %slice-start.3 = ((s8[4587520]{0:T(1024)(128)(4,1)}), s8[393216]{0:T(1024)(128)(4,1)S(1)}, s32[]{:S(2)}) async-start(s8[4587520]{0:T(1024)(128)(4,1)} %bitcast.18), calls=%async_computation.4 | async-start | bytes 786432
  32.2 50.5 %collective-permute-start.12 = (bf16[4,1040,128]{2,1,0:T(8,128)(2,1)S(1)}, bf16[4,1040,128]{2,1,0:T(8,128)(2,1)S(1)}, u32[]{:S(2)}, u32[]{:S(2)}) collective-permute-start(bf16[4,1040,128]{2,1,0:T(8,128)(2,1)S(1)} %get-tuple-element.53), channel_id=1, source_target_pairs={{0,3},{1,0},{2,1},{3,2},{4,7},{5,4},{6,5},{7,6},{8,11},{9,8},{10,9... | collective-permute-start | bytes 3194888 | tf_op jit(solution)/shard_map/ppermute | solution.py:361
  37.0 56.5 %collective-permute-start.17 = (bf16[4,1040,128]{2,1,0:T(8,128)(2,1)S(1)}, bf16[4,1040,128]{2,1,0:T(8,128)(2,1)S(1)}, u32[]{:S(2)}, u32[]{:S(2)}) collective-permute-start(bf16[4,1040,128]{2,1,0:T(8,128)(2,1)S(1)} %get-tuple-element.63), channel_id=1, source_target_pairs={{0,12},{1,13},{2,14},{3,15},{4,0},{5,1},{6,2},{7,3},{8,4},{9,5},{1... | collective-permute-start | bytes 3194888 | tf_op jit(solution)/shard_map/ppermute | solution.py:364
  41.1 52.5 %collective-permute-start.18 = (bf16[4,1040,128]{2,1,0:T(8,128)(2,1)S(1)}, bf16[4,1040,128]{2,1,0:T(8,128)(2,1)S(1)}, u32[]{:S(2)}, u32[]{:S(2)}) collective-permute-start(bf16[4,1040,128]{2,1,0:T(8,128)(2,1)S(1)} %get-tuple-element.64), channel_id=1, source_target_pairs={{0,8},{1,9},{2,10},{3,11},{4,12},{5,13},{6,14},{7,15},{8,0},{9,1},... | collective-permute-start | bytes 3194888 | tf_op jit(solution)/shard_map/ppermute | solution.py:364
  68.1 51.1 %collective-permute-start.7 = (bf16[1,1040,128]{2,1,0:T(8,128)(2,1)S(1)}, bf16[1,1040,128]{2,1,0:T(8,128)(2,1)S(1)}, u32[]{:S(2)}, u32[]{:S(2)}) collective-permute-start(bf16[1,1040,128]{2,1,0:T(8,128)(2,1)S(1)} %get-tuple-element.48), channel_id=1, source_target_pairs={{0,4},{1,5},{2,6},{3,7},{4,8},{5,9},{6,10},{7,11},{8,12},{9,13},{1... | collective-permute-start | bytes 798728 | tf_op jit(solution)/shard_map/ppermute | solution.py:364
  78.8 40.7 %collective-permute-start.8 = (bf16[1,1040,128]{2,1,0:T(8,128)(2,1)S(1)}, bf16[1,1040,128]{2,1,0:T(8,128)(2,1)S(1)}, u32[]{:S(2)}, u32[]{:S(2)}) collective-permute-start(bf16[1,1040,128]{2,1,0:T(8,128)(2,1)S(1)} %get-tuple-element.49), channel_id=1, source_target_pairs={{0,8},{1,9},{2,10},{3,11},{4,12},{5,13},{6,14},{7,15},{8,0},{9,1},... | collective-permute-start | bytes 798728 | tf_op jit(solution)/shard_map/ppermute | solution.py:364
  82.7 39.3 %collective-permute-start.9 = (bf16[1,1040,128]{2,1,0:T(8,128)(2,1)S(1)}, bf16[1,1040,128]{2,1,0:T(8,128)(2,1)S(1)}, u32[]{:S(2)}, u32[]{:S(2)}) collective-permute-start(bf16[1,1040,128]{2,1,0:T(8,128)(2,1)S(1)} %get-tuple-element.50), channel_id=1, source_target_pairs={{0,12},{1,13},{2,14},{3,15},{4,0},{5,1},{6,2},{7,3},{8,4},{9,5},{1... | collective-permute-start | bytes 798728 | tf_op jit(solution)/shard_map/ppermute | solution.py:364
  93.5 24.5 %collective-permute-start.16 = (bf16[4,1040,128]{2,1,0:T(8,128)(2,1)S(1)}, bf16[4,1040,128]{2,1,0:T(8,128)(2,1)S(1)}, u32[]{:S(2)}, u32[]{:S(2)}) collective-permute-start(bf16[4,1040,128]{2,1,0:T(8,128)(2,1)S(1)} %get-tuple-element.62), channel_id=1, source_target_pairs={{0,4},{1,5},{2,6},{3,7},{4,8},{5,9},{6,10},{7,11},{8,12},{9,13},{1... | collective-permute-start | bytes 3194888 | tf_op jit(solution)/shard_map/ppermute | solution.py:364
  93.6 31.6 %collective-permute-start.13 = (bf16[1,1040,128]{2,1,0:T(8,128)(2,1)S(1)}, bf16[1,1040,128]{2,1,0:T(8,128)(2,1)S(1)}, u32[]{:S(2)}, u32[]{:S(2)}) collective-permute-start(bf16[1,1040,128]{2,1,0:T(8,128)(2,1)S(1)} %get-tuple-element.59), channel_id=1, source_target_pairs={{0,1},{1,2},{2,3},{3,0},{4,5},{5,6},{6,7},{7,4},{8,9},{9,10},{10,1... | collective-permute-start | bytes 798728 | tf_op jit(solution)/shard_map/ppermute | solution.py:361
  118.1 10.4 %collective-permute-start.14 = (bf16[1,1040,128]{2,1,0:T(8,128)(2,1)S(1)}, bf16[1,1040,128]{2,1,0:T(8,128)(2,1)S(1)}, u32[]{:S(2)}, u32[]{:S(2)}) collective-permute-start(bf16[1,1040,128]{2,1,0:T(8,128)(2,1)S(1)} %get-tuple-element.60), channel_id=1, source_target_pairs={{0,2},{1,3},{2,0},{3,1},{4,6},{5,7},{6,4},{7,5},{8,10},{9,11},{10,... | collective-permute-start | bytes 798728 | tf_op jit(solution)/shard_map/ppermute | solution.py:361
  119.2 34.9 %collective-permute-start.19 = (bf16[3,1040,128]{2,1,0:T(8,128)(2,1)S(1)}, bf16[3,1040,128]{2,1,0:T(8,128)(2,1)S(1)}, u32[]{:S(2)}, u32[]{:S(2)}) collective-permute-start(bf16[3,1040,128]{2,1,0:T(8,128)(2,1)S(1)} %pad_maximum_fusion), channel_id=1, source_target_pairs={{0,4},{1,5},{2,6},{3,7},{4,8},{5,9},{6,10},{7,11},{8,12},{9,13},{1... | collective-permute-start | bytes 2396168 | tf_op jit(solution)/shard_map/ppermute | solution.py:364
  119.3 36.9 %copy-start.5 = (f32[1,7168,128]{2,1,0:T(8,128)S(1)}, f32[1,7168,128]{2,1,0:T(8,128)}, u32[]{:S(2)}) copy-start(f32[1,7168,128]{2,1,0:T(8,128)} %param.15) | copy-start | bytes 11010052
  119.5 13.2 %collective-permute-start.15 = (bf16[1,1040,128]{2,1,0:T(8,128)(2,1)S(1)}, bf16[1,1040,128]{2,1,0:T(8,128)(2,1)S(1)}, u32[]{:S(2)}, u32[]{:S(2)}) collective-permute-start(bf16[1,1040,128]{2,1,0:T(8,128)(2,1)S(1)} %get-tuple-element.61), channel_id=1, source_target_pairs={{0,3},{1,0},{2,1},{3,2},{4,7},{5,4},{6,5},{7,6},{8,11},{9,8},{10,9... | collective-permute-start | bytes 798728 | tf_op jit(solution)/shard_map/ppermute | solution.py:361
  122.0 37.2 %collective-permute-start.20 = (bf16[3,1040,128]{2,1,0:T(8,128)(2,1)S(1)}, bf16[3,1040,128]{2,1,0:T(8,128)(2,1)S(1)}, u32[]{:S(2)}, u32[]{:S(2)}) collective-permute-start(bf16[3,1040,128]{2,1,0:T(8,128)(2,1)S(1)} %pad_maximum_fusion.1), channel_id=1, source_target_pairs={{0,12},{1,13},{2,14},{3,15},{4,0},{5,1},{6,2},{7,3},{8,4},{9,5},{1... | collective-permute-start | bytes 2396168 | tf_op jit(solution)/shard_map/ppermute | solution.py:364
  125.2 33.9 %collective-permute-start.21 = (bf16[3,1040,128]{2,1,0:T(8,128)(2,1)S(1)}, bf16[3,1040,128]{2,1,0:T(8,128)(2,1)S(1)}, u32[]{:S(2)}, u32[]{:S(2)}) collective-permute-start(bf16[3,1040,128]{2,1,0:T(8,128)(2,1)S(1)} %pad_maximum_fusion.2), channel_id=1, source_target_pairs={{0,1},{1,2},{2,3},{3,0},{4,5},{5,6},{6,7},{7,4},{8,9},{9,10},{10,1... | collective-permute-start | bytes 2396168 | tf_op jit(solution)/shard_map/ppermute | solution.py:361
  128.5 30.7 %collective-permute-start.22 = (bf16[3,1040,128]{2,1,0:T(8,128)(2,1)S(1)}, bf16[3,1040,128]{2,1,0:T(8,128)(2,1)S(1)}, u32[]{:S(2)}, u32[]{:S(2)}) collective-permute-start(bf16[3,1040,128]{2,1,0:T(8,128)(2,1)S(1)} %pad_maximum_fusion.3), channel_id=1, source_target_pairs={{0,3},{1,0},{2,1},{3,2},{4,7},{5,4},{6,5},{7,6},{8,11},{9,8},{10,9... | collective-permute-start | bytes 2396168 | tf_op jit(solution)/shard_map/ppermute | solution.py:361
  132.6 29.0 %collective-permute-start.23 = (bf16[3,1040,128]{2,1,0:T(8,128)(2,1)S(1)}, bf16[3,1040,128]{2,1,0:T(8,128)(2,1)S(1)}, u32[]{:S(2)}, u32[]{:S(2)}) collective-permute-start(bf16[3,1040,128]{2,1,0:T(8,128)(2,1)S(1)} %pad_maximum_fusion.4), channel_id=1, source_target_pairs={{0,8},{1,9},{2,10},{3,11},{4,12},{5,13},{6,14},{7,15},{8,0},{9,1},... | collective-permute-start | bytes 2396168 | tf_op jit(solution)/shard_map/ppermute | solution.py:364
  154.1 13.6 %collective-permute-start.24 = (bf16[3,1040,128]{2,1,0:T(8,128)(2,1)S(1)}, bf16[3,1040,128]{2,1,0:T(8,128)(2,1)S(1)}, u32[]{:S(2)}, u32[]{:S(2)}) collective-permute-start(bf16[3,1040,128]{2,1,0:T(8,128)(2,1)S(1)} %pad_maximum_fusion.5), channel_id=1, source_target_pairs={{0,2},{1,3},{2,0},{3,1},{4,6},{5,7},{6,4},{7,5},{8,10},{9,11},{10,... | collective-permute-start | bytes 2396168 | tf_op jit(solution)/shard_map/ppermute | solution.py:361
  171.0 11.2 %all-to-all-start = ((f32[16,1,128]{2,1,0:T(1,128)}), f32[16,1,128]{2,1,0:T(1,128)S(1)}, u32[]{:S(2)}, u32[]{:S(2)}) async-start(f32[16,1,128]{2,1,0:T(1,128)} %bitcast.9), calls=%async_computation | async-start | bytes 16384 | tf_op jit(solution)/shard_map/all_to_all | solution.py:405
  (5 other events, 7.3 us)

commit v4 on v3

--- a/solution.py
+++ b/solution.py
@@ -264,6 +264,8 @@
 def update_kernel(pieces, last, base_ref, *refs):
     got_refs, (out_ref, *rest) = refs[: len(pieces)], refs[len(pieces) :]
     ids_scr, ids_ref, ids_sem = rest[-3:]
+    if last:
+        result_hbm, (squares_ref, scr, out_ref, result_sem) = out_ref, rest[:4]
     row = 0
     for got_ref, (parts, _) in zip(got_refs, pieces):
         for k in range(parts):
@@ -293,7 +295,8 @@
             lax.fori_loop(0, count, add, 0)
             row += 1
     if last:
-        squares_ref, scr = rest[0], rest[1]
+        result = pltpu.make_async_copy(out_ref, result_hbm, result_sem)
+        result.start()
         scr[...] = jnp.zeros_like(scr)
         for b in range(BLOCKS):
             x = out_ref[b * BLOCK : (b + 1) * BLOCK, :]
@@ -305,6 +308,7 @@
             precision=lax.Precision.HIGHEST,
             preferred_element_type=jnp.float32,
         )
+        result.wait()
 
 
 def update(base, got, pieces, last):
@@ -313,13 +317,14 @@
     scratch = []
     if last:
         out_shape.append(jax.ShapeDtypeStruct((16, LANES), jnp.float32))
-        scratch.append(pltpu.VMEM((LANES, LANES), jnp.float32))
+        scratch += [pltpu.VMEM((LANES, LANES), jnp.float32), pltpu.VMEM(base.shape, jnp.float32)]
+        scratch.append(pltpu.SemaphoreType.DMA)
     rows = -(-sum(parts for parts, _ in pieces) // 8) * 8
     return pl.pallas_call(
         functools.partial(update_kernel, pieces, last),
         out_shape=out_shape,
         in_specs=[vmem] * (1 + len(got)),
-        out_specs=[vmem] * len(out_shape),
+        out_specs=[pl.BlockSpec(memory_space=pltpu.HBM), vmem] if last else [vmem],
         scratch_shapes=[
             *scratch,
             pltpu.VMEM((rows, LANES), jnp.int32),

time: 183 us -> 184 us (level)
  no operation moved by 1% of the time
where the time goes in v4:
time: 184 us; the launch traced here: 183 us
  waiting for transfers between devices  85.9 us (47%)
  Pallas kernels  48.7 us (26%)
  starting transfers between devices  39.3 us (21%)
  local copies, waits for them, and re-layouts  6.97 us (4%)
    ppermute x9, waiting for transfers between devices, along_z(): return lax.ppermute(x, 'dp', shift(workers, k, 0))  54.3 us
    pallas_call x1, Pallas kernels, norms(): pl.pallas_call(norms_kernel, out_shape=jax.ShapeDtypeStruct((BLOCKS, 1, L...  26.8 us
    ppermute x9, waiting for transfers between devices, along_y(): return lax.ppermute(x, 'dp', shift(workers, 0, k))  21.6 us
    ppermute x9, starting transfers between devices, along_z(): return lax.ppermute(x, 'dp', shift(workers, k, 0))  14.1 us
    ppermute x9, starting transfers between devices, along_y(): return lax.ppermute(x, 'dp', shift(workers, 0, k))  13.4 us
    pallas_call x3, Pallas kernels, update(): pl.pallas_call(functools.partial(update_kernel, pieces, last), out_shape=...  9.31 us
    ppermute x7, starting transfers between devices, local(): arrived[r] = lax.ppermute(tables[r], 'expert', cross(experts, r))  8.19 us
    all_to_all x1, waiting for transfers between devices, local(): exchange(squares.reshape(workers, 1, LANES), 'dp').reshape(workers, LANES)  7.08 us
  transfers between devices with their start and end apart: 26, of which 11 were waited for; matrix products, arithmetic and copies ran while one was open for 1% of the time, Pallas kernels for 21%

profile of v4, /device:TPU:0, one launch (start us, length us, event | category | flops | bytes accessed | tf_op | source)
XLA Modules:
  0.0 183.4 jit_solution(17985919229562228638)
XLA Ops:
  0.6 2.7 %plan.1 = (bf16[40,2048]{1,0:T(8,128)(2,1)}, bf16[40,2048]{1,0:T(8,128)(2,1)}, bf16[40,2048]{1,0:T(8,128)(2,1)}, bf16[40,2048]{1,0:T(8,128)(2,1)}, bf16[40,2048]...) custom-call(s32[2,128]{1,0:T(2,128)} %bitcast.23, ...), custom_call_target="tpu_custom_call" | custom-call | flops 200000000 | bytes 2000000 | tf_op jit(solution)/shard_map/plan/pallas_call | solution.py:87
  3.3 1.7 collective-permute-start.1
  6.2 1.6 collective-permute-start.3
  7.9 1.6 collective-permute-start.4
  9.5 1.7 collective-permute-start.5
  12.2 2.3 %copy-done = bf16[1,1,8,40,7168]{4,3,2,1,0:T(8,128)(2,1)S(1)} copy-done((bf16[1,1,8,40,7168]{4,3,2,1,0:T(8,128)(2,1)S(1)}, bf16[1,1,8,40,7168]{4,3,2,1,0:T(8,128)(2,1)}, u32[]{:S(2)}) %copy-start) | copy-done | bytes 4587544
  14.5 2.3 %copy-done.1 = bf16[1,1,8,40,7168]{4,3,2,1,0:T(8,128)(2,1)S(1)} copy-done((bf16[1,1,8,40,7168]{4,3,2,1,0:T(8,128)(2,1)S(1)}, bf16[1,1,8,40,7168]{4,3,2,1,0:T(8,128)(2,1)}, u32[]{:S(2)}) %copy-start.1) | copy-done | bytes 4587544
  16.8 1.3 copy-done.2
  18.8 2.3 %fetch.1 = (bf16[320,2048]{1,0:T(8,128)(2,1)S(1)}, bf16[640,1024]{1,0:T(8,128)(2,1)S(1)}, bf16[640,1024]{1,0:T(8,128)(2,1)S(1)}) custom-call(s32[16,128]{1,0:T(8,128)S(1)} %copy-done.4, bf16[320,7168]{1,0:T(8,128)(2,1)S(1)} %bitcast.13, bf16[320,7168]{1,0:T(8,128)(2,1)S(1)} %bitcast.17, bf16[320,2048]{1,0:T(8,128)(2,1)S(1)} %bitcast.21), custom_call_target="tpu_custom_call" | custom-call | flops 100000000 | bytes 6600000 | tf_op jit(solution)/shard_map/fetch/pallas_call | solution.py:139
  24.1 3.5 %products.2 = (bf16[1,1040,128]{2,1,0:T(8,128)(2,1)S(1)}, bf16[1,1040,128]{2,1,0:T(8,128)(2,1)S(1)}, bf16[1,1040,128]{2,1,0:T(8,128)(2,1)S(1)}, bf16[1,1040,128]...) custom-call(s32[1,128]{1,0:T(1,128)S(1)} %copy-done.6, ...), custom_call_target="tpu_custom_call" | custom-call | flops 2684354560 | bytes 8000000 | tf_op jit(solution)/shard_map/products/pallas_call | solution.py:208
  27.6 1.6 collective-permute-start.10
  29.3 2.9 %collective-permute-start.11 = (bf16[4,1040,128]{2,1,0:T(8,128)(2,1)S(1)}, bf16[4,1040,128]{2,1,0:T(8,128)(2,1)S(1)}, u32[]{:S(2)}, u32[]{:S(2)}) collective-permute-start(bf16[4,1040,128]{2,1,0:T(8,128)(2,1)S(1)} %get-tuple-element.52), channel_id=1, source_target_pairs={{0,2},{1,3},{2,0},{3,1},{4,6},{5,7},{6,4},{7,5},{8,10},{9,11},{10,... | collective-permute-start | bytes 3194888 | tf_op jit(solution)/shard_map/ppermute | solution.py:366
  32.2 1.3 collective-permute-start.12
  33.5 3.5 %products.3 = (bf16[1,1040,128]{2,1,0:T(8,128)(2,1)S(1)}, bf16[1,1040,128]{2,1,0:T(8,128)(2,1)S(1)}, bf16[1,1040,128]{2,1,0:T(8,128)(2,1)S(1)}, bf16[1,1040,128]...) custom-call(s32[1,128]{1,0:T(1,128)S(1)} %copy-done.6, ...), custom_call_target="tpu_custom_call" | custom-call | flops 2684354560 | bytes 8000000 | tf_op jit(solution)/shard_map/products/pallas_call | solution.py:208
  37.0 4.1 %collective-permute-start.17 = (bf16[4,1040,128]{2,1,0:T(8,128)(2,1)S(1)}, bf16[4,1040,128]{2,1,0:T(8,128)(2,1)S(1)}, u32[]{:S(2)}, u32[]{:S(2)}) collective-permute-start(bf16[4,1040,128]{2,1,0:T(8,128)(2,1)S(1)} %get-tuple-element.63), channel_id=1, source_target_pairs={{0,12},{1,13},{2,14},{3,15},{4,0},{5,1},{6,2},{7,3},{8,4},{9,5},{1... | collective-permute-start | bytes 3194888 | tf_op jit(solution)/shard_map/ppermute | solution.py:369
  41.3 26.8 %norms.1 = f32[56,1,128]{2,1,0:T(1,128)S(1)} custom-call(bf16[320,7168]{1,0:T(8,128)(2,1)S(1)} %bitcast.16, bf16[320,7168]{1,0:T(8,128)(2,1)S(1)} %bitcast.20, bf16[640,2048]{1,0:T(8,128)(2,1)S(1)} %arrange.1.right_ref), custom_call_target="tpu_custom_call" | custom-call | flops 18790481920 | bytes 11775040 | tf_op jit(solution)/shard_map/norms/pallas_call | solution.py:243
  69.3 9.5 %collective-permute-done.11.refs_6_ = bf16[4,1040,128]{2,1,0:T(8,128)(2,1)S(1)} collective-permute-done((bf16[4,1040,128]{2,1,0:T(8,128)(2,1)S(1)}, bf16[4,1040,128]{2,1,0:T(8,128)(2,1)S(1)}, u32[]{:S(2)}, u32[]{:S(2)}) %collective-permute-start.11) | collective-permute-done | bytes 1064992 | tf_op jit(solution)/shard_map/ppermute | solution.py:366
  78.8 3.9 %collective-permute-start.8 = (bf16[1,1040,128]{2,1,0:T(8,128)(2,1)S(1)}, bf16[1,1040,128]{2,1,0:T(8,128)(2,1)S(1)}, u32[]{:S(2)}, u32[]{:S(2)}) collective-permute-start(bf16[1,1040,128]{2,1,0:T(8,128)(2,1)S(1)} %get-tuple-element.49), channel_id=1, source_target_pairs={{0,8},{1,9},{2,10},{3,11},{4,12},{5,13},{6,14},{7,15},{8,0},{9,1},... | collective-permute-start | bytes 798728 | tf_op jit(solution)/shard_map/ppermute | solution.py:369
  83.5 10.1 %collective-permute-done.17.refs_12_ = bf16[4,1040,128]{2,1,0:T(8,128)(2,1)S(1)} collective-permute-done((bf16[4,1040,128]{2,1,0:T(8,128)(2,1)S(1)}, bf16[4,1040,128]{2,1,0:T(8,128)(2,1)S(1)}, u32[]{:S(2)}, u32[]{:S(2)}) %collective-permute-start.17) | collective-permute-done | bytes 1064992 | tf_op jit(solution)/shard_map/ppermute | solution.py:369
  94.5 23.5 %collective-permute-done.16.refs_11_ = bf16[4,1040,128]{2,1,0:T(8,128)(2,1)S(1)} collective-permute-done((bf16[4,1040,128]{2,1,0:T(8,128)(2,1)S(1)}, bf16[4,1040,128]{2,1,0:T(8,128)(2,1)S(1)}, u32[]{:S(2)}, u32[]{:S(2)}) %collective-permute-start.16) | collective-permute-done | bytes 1064992 | tf_op jit(solution)/shard_map/ppermute | solution.py:369
  119.5 2.6 %collective-permute-start.15 = (bf16[1,1040,128]{2,1,0:T(8,128)(2,1)S(1)}, bf16[1,1040,128]{2,1,0:T(8,128)(2,1)S(1)}, u32[]{:S(2)}, u32[]{:S(2)}) collective-permute-start(bf16[1,1040,128]{2,1,0:T(8,128)(2,1)S(1)} %get-tuple-element.61), channel_id=1, source_target_pairs={{0,3},{1,0},{2,1},{3,2},{4,7},{5,4},{6,5},{7,6},{8,11},{9,8},{10,9... | collective-permute-start | bytes 798728 | tf_op jit(solution)/shard_map/ppermute | solution.py:366
  122.0 3.2 %collective-permute-start.20 = (bf16[3,1040,128]{2,1,0:T(8,128)(2,1)S(1)}, bf16[3,1040,128]{2,1,0:T(8,128)(2,1)S(1)}, u32[]{:S(2)}, u32[]{:S(2)}) collective-permute-start(bf16[3,1040,128]{2,1,0:T(8,128)(2,1)S(1)} %pad_maximum_fusion.1), channel_id=1, source_target_pairs={{0,12},{1,13},{2,14},{3,15},{4,0},{5,1},{6,2},{7,3},{8,4},{9,5},{1... | collective-permute-start | bytes 2396168 | tf_op jit(solution)/shard_map/ppermute | solution.py:369
  125.3 3.2 %collective-permute-done.14.refs_9_ = bf16[1,1040,128]{2,1,0:T(8,128)(2,1)S(1)} collective-permute-done((bf16[1,1040,128]{2,1,0:T(8,128)(2,1)S(1)}, bf16[1,1040,128]{2,1,0:T(8,128)(2,1)S(1)}, u32[]{:S(2)}, u32[]{:S(2)}) %collective-permute-start.14) | collective-permute-done | bytes 266272 | tf_op jit(solution)/shard_map/ppermute | solution.py:366
  129.8 2.8 %collective-permute-done.15.refs_10_ = bf16[1,1040,128]{2,1,0:T(8,128)(2,1)S(1)} collective-permute-done((bf16[1,1040,128]{2,1,0:T(8,128)(2,1)S(1)}, bf16[1,1040,128]{2,1,0:T(8,128)(2,1)S(1)}, u32[]{:S(2)}, u32[]{:S(2)}) %collective-permute-start.15) | collective-permute-done | bytes 266272 | tf_op jit(solution)/shard_map/ppermute | solution.py:366
  133.4 20.7 %collective-permute-done.19.refs_0_ = bf16[3,1040,128]{2,1,0:T(8,128)(2,1)S(1)} collective-permute-done((bf16[3,1040,128]{2,1,0:T(8,128)(2,1)S(1)}, bf16[3,1040,128]{2,1,0:T(8,128)(2,1)S(1)}, u32[]{:S(2)}, u32[]{:S(2)}) %collective-permute-start.19) | collective-permute-done | bytes 798752 | tf_op jit(solution)/shard_map/ppermute | solution.py:369
  154.1 2.2 %collective-permute-start.24 = (bf16[3,1040,128]{2,1,0:T(8,128)(2,1)S(1)}, bf16[3,1040,128]{2,1,0:T(8,128)(2,1)S(1)}, u32[]{:S(2)}, u32[]{:S(2)}) collective-permute-start(bf16[3,1040,128]{2,1,0:T(8,128)(2,1)S(1)} %pad_maximum_fusion.5), channel_id=1, source_target_pairs={{0,2},{1,3},{2,0},{3,1},{4,6},{5,7},{6,4},{7,5},{8,10},{9,11},{10,... | collective-permute-start | bytes 2396168 | tf_op jit(solution)/shard_map/ppermute | solution.py:366
  156.2 2.9 %update.2.base_ref = f32[7168,128]{1,0:T(8,128)S(1)} custom-call(f32[7168,128]{1,0:T(8,128)S(1)} %bitcast.22, bf16[1,1040,128]{2,1,0:T(8,128)(2,1)S(1)} %get-tuple-element.47.refs_0_, bf16[1,1040,128]{2,1,0:T(8,128)(2,1)S(1)} %collective-permute-done.7.refs_1_, bf16[1,1040,128]{2,1,0:T(8,128)(2,1)S(1)} %collective-permute-done.8.refs_2_, ...), custom_call_target="tpu_custom_call" | custom-call | flops 5000000000 | bytes 16000000 | tf_op jit(solution)/shard_map/update/pallas_call | solution.py:323
  159.2 2.4 %update.3.base_ref = f32[7168,128]{1,0:T(8,128)S(1)} custom-call(f32[7168,128]{1,0:T(8,128)S(1)} %update.2.base_ref, bf16[3,1040,128]{2,1,0:T(8,128)(2,1)S(1)} %collective-permute-done.19.refs_0_, bf16[3,1040,128]{2,1,0:T(8,128)(2,1)S(1)} %collective-permute-done.20.refs_1_, bf16[3,1040,128]{2,1,0:T(8,128)(2,1)S(1)} %collective-permute-done.21.refs_2_, ...), custom_call_target="tpu_custom_call" | custom-call | flops 5000000000 | bytes 16000000 | tf_op jit(solution)/shard_map/update/pallas_call | solution.py:323
  161.7 6.0 %collective-permute-done.24.refs_1_ = bf16[3,1040,128]{2,1,0:T(8,128)(2,1)S(1)} collective-permute-done((bf16[3,1040,128]{2,1,0:T(8,128)(2,1)S(1)}, bf16[3,1040,128]{2,1,0:T(8,128)(2,1)S(1)}, u32[]{:S(2)}, u32[]{:S(2)}) %collective-permute-start.24) | collective-permute-done | bytes 798752 | tf_op jit(solution)/shard_map/ppermute | solution.py:366
  167.7 3.9 %update_last.1 = (f32[7168,128]{1,0:T(8,128)}, f32[16,128]{1,0:T(8,128)}) custom-call(f32[7168,128]{1,0:T(8,128)S(1)} %update.3.base_ref, bf16[3,1040,128]{2,1,0:T(8,128)(2,1)S(1)} %collective-permute-done.23.refs_0_, bf16[3,1040,128]{2,1,0:T(8,128)(2,1)S(1)} %collective-permute-done.24.refs_1_), custom_call_target="tpu_custom_call" | custom-call | flops 5000000000 | bytes 16000000 | tf_op jit(solution)/shard_map/update_last/pallas_call | solution.py:323
  171.6 3.6 %all-to-all-start = ((f32[16,1,128]{2,1,0:T(1,128)}), f32[16,1,128]{2,1,0:T(1,128)S(1)}, u32[]{:S(2)}, u32[]{:S(2)}) async-start(f32[16,1,128]{2,1,0:T(1,128)} %bitcast.9), calls=%async_computation | async-start | bytes 16384 | tf_op jit(solution)/shard_map/all_to_all | solution.py:410
  175.8 7.1 %all-to-all-done = f32[16,1,128]{2,1,0:T(1,128)S(1)} async-done(((f32[16,1,128]{2,1,0:T(1,128)}), f32[16,1,128]{2,1,0:T(1,128)S(1)}, u32[]{:S(2)}, u32[]{:S(2)}) %all-to-all-start) | async-done | bytes 8224 | tf_op jit(solution)/shard_map/all_to_all | solution.py:410
  (67 shorter events, 13.5 us)
Async XLA Ops:
  3.3 6.1 %collective-permute-start = (bf16[40,2048]{1,0:T(8,128)(2,1)}, bf16[40,2048]{1,0:T(8,128)(2,1)S(1)}, u32[]{:S(2)}, u32[]{:S(2)}) collective-permute-start(bf16[40,2048]{1,0:T(8,128)(2,1)} %get-tuple-element.39), channel_id=1, source_target_pairs={{0,16},{16,0},{32,48},{48,32},{64,80},{80,64},{96,112},{112,96},{1... | collective-permute-start | bytes 491528 | tf_op jit(solution)/shard_map/ppermute | solution.py:359
  3.3 8.6 %collective-permute-start.1 = (bf16[40,2048]{1,0:T(8,128)(2,1)}, bf16[40,2048]{1,0:T(8,128)(2,1)S(1)}, u32[]{:S(2)}, u32[]{:S(2)}) collective-permute-start(bf16[40,2048]{1,0:T(8,128)(2,1)} %get-tuple-element.40), channel_id=1, source_target_pairs={{0,32},{16,48},{32,64},{48,80},{64,96},{80,112},{96,0},{112,16},{1... | collective-permute-start | bytes 491528 | tf_op jit(solution)/shard_map/ppermute | solution.py:359
  5.0 16.2 %collective-permute-start.2 = (bf16[40,2048]{1,0:T(8,128)(2,1)}, bf16[40,2048]{1,0:T(8,128)(2,1)S(1)}, u32[]{:S(2)}, u32[]{:S(2)}) collective-permute-start(bf16[40,2048]{1,0:T(8,128)(2,1)} %get-tuple-element.41), channel_id=1, source_target_pairs={{0,48},{16,32},{32,80},{48,64},{64,112},{80,96},{96,16},{112,0},{1... | collective-permute-start | bytes 491528 | tf_op jit(solution)/shard_map/ppermute | solution.py:359
  6.2 14.9 %collective-permute-start.3 = (bf16[40,2048]{1,0:T(8,128)(2,1)}, bf16[40,2048]{1,0:T(8,128)(2,1)S(1)}, u32[]{:S(2)}, u32[]{:S(2)}) collective-permute-start(bf16[40,2048]{1,0:T(8,128)(2,1)} %get-tuple-element.42), channel_id=1, source_target_pairs={{0,64},{16,80},{32,96},{48,112},{64,0},{80,16},{96,32},{112,48},{1... | collective-permute-start | bytes 491528 | tf_op jit(solution)/shard_map/ppermute | solution.py:359
  7.9 14.6 %collective-permute-start.4 = (bf16[40,2048]{1,0:T(8,128)(2,1)}, bf16[40,2048]{1,0:T(8,128)(2,1)S(1)}, u32[]{:S(2)}, u32[]{:S(2)}) collective-permute-start(bf16[40,2048]{1,0:T(8,128)(2,1)} %get-tuple-element.43), channel_id=1, source_target_pairs={{0,80},{16,64},{32,112},{48,96},{64,16},{80,0},{96,48},{112,32},{1... | collective-permute-start | bytes 491528 | tf_op jit(solution)/shard_map/ppermute | solution.py:359
  9.5 13.0 %collective-permute-start.5 = (bf16[40,2048]{1,0:T(8,128)(2,1)}, bf16[40,2048]{1,0:T(8,128)(2,1)S(1)}, u32[]{:S(2)}, u32[]{:S(2)}) collective-permute-start(bf16[40,2048]{1,0:T(8,128)(2,1)} %get-tuple-element.44), channel_id=1, source_target_pairs={{0,96},{16,112},{32,0},{48,16},{64,32},{80,48},{96,64},{112,80},{1... | collective-permute-start | bytes 491528 | tf_op jit(solution)/shard_map/ppermute | solution.py:359
  11.9 11.6 %collective-permute-start.6 = (bf16[40,2048]{1,0:T(8,128)(2,1)}, bf16[40,2048]{1,0:T(8,128)(2,1)S(1)}, u32[]{:S(2)}, u32[]{:S(2)}) collective-permute-start(bf16[40,2048]{1,0:T(8,128)(2,1)} %get-tuple-element.45), channel_id=1, source_target_pairs={{0,112},{16,96},{32,16},{48,0},{64,48},{80,32},{96,80},{112,64},{1... | collective-permute-start | bytes 491528 | tf_op jit(solution)/shard_map/ppermute | solution.py:359
  18.8 4.7 %copy-start.3 = (bf16[40,2048]{1,0:T(8,128)(2,1)S(1)}, bf16[40,2048]{1,0:T(8,128)(2,1)}, u32[]{:S(2)}) copy-start(bf16[40,2048]{1,0:T(8,128)(2,1)} %get-tuple-element.38.refs_0_) | copy-start | bytes 491524
  24.1 17.1 %slice-start = ((s8[4587520]{0:T(1024)(128)(4,1)}), s8[4194304]{0:T(1024)(128)(4,1)S(1)}, s32[]{:S(2)}) async-start(s8[4587520]{0:T(1024)(128)(4,1)} %bitcast.14), calls=%async_computation.1 | async-start | bytes 8388608
  24.1 17.1 %slice-start.2 = ((s8[4587520]{0:T(1024)(128)(4,1)}), s8[4194304]{0:T(1024)(128)(4,1)S(1)}, s32[]{:S(2)}) async-start(s8[4587520]{0:T(1024)(128)(4,1)} %bitcast.18), calls=%async_computation.3 | async-start | bytes 8388608
  27.6 40.5 %collective-permute-start.10 = (bf16[4,1040,128]{2,1,0:T(8,128)(2,1)S(1)}, bf16[4,1040,128]{2,1,0:T(8,128)(2,1)S(1)}, u32[]{:S(2)}, u32[]{:S(2)}) collective-permute-start(bf16[4,1040,128]{2,1,0:T(8,128)(2,1)S(1)} %get-tuple-element.51), channel_id=1, source_target_pairs={{0,1},{1,2},{2,3},{3,0},{4,5},{5,6},{6,7},{7,4},{8,9},{9,10},{10,1... | collective-permute-start | bytes 3194888 | tf_op jit(solution)/shard_map/ppermute | solution.py:366
  29.3 49.5 %collective-permute-start.11 = (bf16[4,1040,128]{2,1,0:T(8,128)(2,1)S(1)}, bf16[4,1040,128]{2,1,0:T(8,128)(2,1)S(1)}, u32[]{:S(2)}, u32[]{:S(2)}) collective-permute-start(bf16[4,1040,128]{2,1,0:T(8,128)(2,1)S(1)} %get-tuple-element.52), channel_id=1, source_target_pairs={{0,2},{1,3},{2,0},{3,1},{4,6},{5,7},{6,4},{7,5},{8,10},{9,11},{10,... | collective-permute-start | bytes 3194888 | tf_op jit(solution)/shard_map/ppermute | solution.py:366
  32.2 9.1 %slice-start.1 = ((s8[4587520]{0:T(1024)(128)(4,1)}), s8[393216]{0:T(1024)(128)(4,1)S(1)}, s32[]{:S(2)}) async-start(s8[4587520]{0:T(1024)(128)(4,1)} %bitcast.14), calls=%async_computation.2 | async-start | bytes 786432
  32.2 9.1 %slice-start.3 = ((s8[4587520]{0:T(1024)(128)(4,1)}), s8[393216]{0:T(1024)(128)(4,1)S(1)}, s32[]{:S(2)}) async-start(s8[4587520]{0:T(1024)(128)(4,1)} %bitcast.18), calls=%async_computation.4 | async-start | bytes 786432
  32.2 50.5 %collective-permute-start.12 = (bf16[4,1040,128]{2,1,0:T(8,128)(2,1)S(1)}, bf16[4,1040,128]{2,1,0:T(8,128)(2,1)S(1)}, u32[]{:S(2)}, u32[]{:S(2)}) collective-permute-start(bf16[4,1040,128]{2,1,0:T(8,128)(2,1)S(1)} %get-tuple-element.53), channel_id=1, source_target_pairs={{0,3},{1,0},{2,1},{3,2},{4,7},{5,4},{6,5},{7,6},{8,11},{9,8},{10,9... | collective-permute-start | bytes 3194888 | tf_op jit(solution)/shard_map/ppermute | solution.py:366
  37.0 56.5 %collective-permute-start.17 = (bf16[4,1040,128]{2,1,0:T(8,128)(2,1)S(1)}, bf16[4,1040,128]{2,1,0:T(8,128)(2,1)S(1)}, u32[]{:S(2)}, u32[]{:S(2)}) collective-permute-start(bf16[4,1040,128]{2,1,0:T(8,128)(2,1)S(1)} %get-tuple-element.63), channel_id=1, source_target_pairs={{0,12},{1,13},{2,14},{3,15},{4,0},{5,1},{6,2},{7,3},{8,4},{9,5},{1... | collective-permute-start | bytes 3194888 | tf_op jit(solution)/shard_map/ppermute | solution.py:369
  41.1 52.5 %collective-permute-start.18 = (bf16[4,1040,128]{2,1,0:T(8,128)(2,1)S(1)}, bf16[4,1040,128]{2,1,0:T(8,128)(2,1)S(1)}, u32[]{:S(2)}, u32[]{:S(2)}) collective-permute-start(bf16[4,1040,128]{2,1,0:T(8,128)(2,1)S(1)} %get-tuple-element.64), channel_id=1, source_target_pairs={{0,8},{1,9},{2,10},{3,11},{4,12},{5,13},{6,14},{7,15},{8,0},{9,1},... | collective-permute-start | bytes 3194888 | tf_op jit(solution)/shard_map/ppermute | solution.py:369
  68.1 51.1 %collective-permute-start.7 = (bf16[1,1040,128]{2,1,0:T(8,128)(2,1)S(1)}, bf16[1,1040,128]{2,1,0:T(8,128)(2,1)S(1)}, u32[]{:S(2)}, u32[]{:S(2)}) collective-permute-start(bf16[1,1040,128]{2,1,0:T(8,128)(2,1)S(1)} %get-tuple-element.48), channel_id=1, source_target_pairs={{0,4},{1,5},{2,6},{3,7},{4,8},{5,9},{6,10},{7,11},{8,12},{9,13},{1... | collective-permute-start | bytes 798728 | tf_op jit(solution)/shard_map/ppermute | solution.py:369
  78.8 40.7 %collective-permute-start.8 = (bf16[1,1040,128]{2,1,0:T(8,128)(2,1)S(1)}, bf16[1,1040,128]{2,1,0:T(8,128)(2,1)S(1)}, u32[]{:S(2)}, u32[]{:S(2)}) collective-permute-start(bf16[1,1040,128]{2,1,0:T(8,128)(2,1)S(1)} %get-tuple-element.49), channel_id=1, source_target_pairs={{0,8},{1,9},{2,10},{3,11},{4,12},{5,13},{6,14},{7,15},{8,0},{9,1},... | collective-permute-start | bytes 798728 | tf_op jit(solution)/shard_map/ppermute | solution.py:369
  82.7 39.3 %collective-permute-start.9 = (bf16[1,1040,128]{2,1,0:T(8,128)(2,1)S(1)}, bf16[1,1040,128]{2,1,0:T(8,128)(2,1)S(1)}, u32[]{:S(2)}, u32[]{:S(2)}) collective-permute-start(bf16[1,1040,128]{2,1,0:T(8,128)(2,1)S(1)} %get-tuple-element.50), channel_id=1, source_target_pairs={{0,12},{1,13},{2,14},{3,15},{4,0},{5,1},{6,2},{7,3},{8,4},{9,5},{1... | collective-permute-start | bytes 798728 | tf_op jit(solution)/shard_map/ppermute | solution.py:369
  93.5 24.5 %collective-permute-start.16 = (bf16[4,1040,128]{2,1,0:T(8,128)(2,1)S(1)}, bf16[4,1040,128]{2,1,0:T(8,128)(2,1)S(1)}, u32[]{:S(2)}, u32[]{:S(2)}) collective-permute-start(bf16[4,1040,128]{2,1,0:T(8,128)(2,1)S(1)} %get-tuple-element.62), channel_id=1, source_target_pairs={{0,4},{1,5},{2,6},{3,7},{4,8},{5,9},{6,10},{7,11},{8,12},{9,13},{1... | collective-permute-start | bytes 3194888 | tf_op jit(solution)/shard_map/ppermute | solution.py:369
  93.6 31.6 %collective-permute-start.13 = (bf16[1,1040,128]{2,1,0:T(8,128)(2,1)S(1)}, bf16[1,1040,128]{2,1,0:T(8,128)(2,1)S(1)}, u32[]{:S(2)}, u32[]{:S(2)}) collective-permute-start(bf16[1,1040,128]{2,1,0:T(8,128)(2,1)S(1)} %get-tuple-element.59), channel_id=1, source_target_pairs={{0,1},{1,2},{2,3},{3,0},{4,5},{5,6},{6,7},{7,4},{8,9},{9,10},{10,1... | collective-permute-start | bytes 798728 | tf_op jit(solution)/shard_map/ppermute | solution.py:366
  118.1 10.4 %collective-permute-start.14 = (bf16[1,1040,128]{2,1,0:T(8,128)(2,1)S(1)}, bf16[1,1040,128]{2,1,0:T(8,128)(2,1)S(1)}, u32[]{:S(2)}, u32[]{:S(2)}) collective-permute-start(bf16[1,1040,128]{2,1,0:T(8,128)(2,1)S(1)} %get-tuple-element.60), channel_id=1, source_target_pairs={{0,2},{1,3},{2,0},{3,1},{4,6},{5,7},{6,4},{7,5},{8,10},{9,11},{10,... | collective-permute-start | bytes 798728 | tf_op jit(solution)/shard_map/ppermute | solution.py:366
  119.2 34.9 %collective-permute-start.19 = (bf16[3,1040,128]{2,1,0:T(8,128)(2,1)S(1)}, bf16[3,1040,128]{2,1,0:T(8,128)(2,1)S(1)}, u32[]{:S(2)}, u32[]{:S(2)}) collective-permute-start(bf16[3,1040,128]{2,1,0:T(8,128)(2,1)S(1)} %pad_maximum_fusion), channel_id=1, source_target_pairs={{0,4},{1,5},{2,6},{3,7},{4,8},{5,9},{6,10},{7,11},{8,12},{9,13},{1... | collective-permute-start | bytes 2396168 | tf_op jit(solution)/shard_map/ppermute | solution.py:369
  119.3 36.9 %copy-start.5 = (f32[1,7168,128]{2,1,0:T(8,128)S(1)}, f32[1,7168,128]{2,1,0:T(8,128)}, u32[]{:S(2)}) copy-start(f32[1,7168,128]{2,1,0:T(8,128)} %param.15) | copy-start | bytes 11010052
  119.5 13.2 %collective-permute-start.15 = (bf16[1,1040,128]{2,1,0:T(8,128)(2,1)S(1)}, bf16[1,1040,128]{2,1,0:T(8,128)(2,1)S(1)}, u32[]{:S(2)}, u32[]{:S(2)}) collective-permute-start(bf16[1,1040,128]{2,1,0:T(8,128)(2,1)S(1)} %get-tuple-element.61), channel_id=1, source_target_pairs={{0,3},{1,0},{2,1},{3,2},{4,7},{5,4},{6,5},{7,6},{8,11},{9,8},{10,9... | collective-permute-start | bytes 798728 | tf_op jit(solution)/shard_map/ppermute | solution.py:366
  122.0 37.2 %collective-permute-start.20 = (bf16[3,1040,128]{2,1,0:T(8,128)(2,1)S(1)}, bf16[3,1040,128]{2,1,0:T(8,128)(2,1)S(1)}, u32[]{:S(2)}, u32[]{:S(2)}) collective-permute-start(bf16[3,1040,128]{2,1,0:T(8,128)(2,1)S(1)} %pad_maximum_fusion.1), channel_id=1, source_target_pairs={{0,12},{1,13},{2,14},{3,15},{4,0},{5,1},{6,2},{7,3},{8,4},{9,5},{1... | collective-permute-start | bytes 2396168 | tf_op jit(solution)/shard_map/ppermute | solution.py:369
  125.2 33.9 %collective-permute-start.21 = (bf16[3,1040,128]{2,1,0:T(8,128)(2,1)S(1)}, bf16[3,1040,128]{2,1,0:T(8,128)(2,1)S(1)}, u32[]{:S(2)}, u32[]{:S(2)}) collective-permute-start(bf16[3,1040,128]{2,1,0:T(8,128)(2,1)S(1)} %pad_maximum_fusion.2), channel_id=1, source_target_pairs={{0,1},{1,2},{2,3},{3,0},{4,5},{5,6},{6,7},{7,4},{8,9},{9,10},{10,1... | collective-permute-start | bytes 2396168 | tf_op jit(solution)/shard_map/ppermute | solution.py:366
  128.5 30.7 %collective-permute-start.22 = (bf16[3,1040,128]{2,1,0:T(8,128)(2,1)S(1)}, bf16[3,1040,128]{2,1,0:T(8,128)(2,1)S(1)}, u32[]{:S(2)}, u32[]{:S(2)}) collective-permute-start(bf16[3,1040,128]{2,1,0:T(8,128)(2,1)S(1)} %pad_maximum_fusion.3), channel_id=1, source_target_pairs={{0,3},{1,0},{2,1},{3,2},{4,7},{5,4},{6,5},{7,6},{8,11},{9,8},{10,9... | collective-permute-start | bytes 2396168 | tf_op jit(solution)/shard_map/ppermute | solution.py:366
  132.6 29.0 %collective-permute-start.23 = (bf16[3,1040,128]{2,1,0:T(8,128)(2,1)S(1)}, bf16[3,1040,128]{2,1,0:T(8,128)(2,1)S(1)}, u32[]{:S(2)}, u32[]{:S(2)}) collective-permute-start(bf16[3,1040,128]{2,1,0:T(8,128)(2,1)S(1)} %pad_maximum_fusion.4), channel_id=1, source_target_pairs={{0,8},{1,9},{2,10},{3,11},{4,12},{5,13},{6,14},{7,15},{8,0},{9,1},... | collective-permute-start | bytes 2396168 | tf_op jit(solution)/shard_map/ppermute | solution.py:369
  154.1 13.6 %collective-permute-start.24 = (bf16[3,1040,128]{2,1,0:T(8,128)(2,1)S(1)}, bf16[3,1040,128]{2,1,0:T(8,128)(2,1)S(1)}, u32[]{:S(2)}, u32[]{:S(2)}) collective-permute-start(bf16[3,1040,128]{2,1,0:T(8,128)(2,1)S(1)} %pad_maximum_fusion.5), channel_id=1, source_target_pairs={{0,2},{1,3},{2,0},{3,1},{4,6},{5,7},{6,4},{7,5},{8,10},{9,11},{10,... | collective-permute-start | bytes 2396168 | tf_op jit(solution)/shard_map/ppermute | solution.py:366
  171.6 11.2 %all-to-all-start = ((f32[16,1,128]{2,1,0:T(1,128)}), f32[16,1,128]{2,1,0:T(1,128)S(1)}, u32[]{:S(2)}, u32[]{:S(2)}) async-start(f32[16,1,128]{2,1,0:T(1,128)} %bitcast.9), calls=%async_computation | async-start | bytes 16384 | tf_op jit(solution)/shard_map/all_to_all | solution.py:410
  (5 other events, 7.3 us)
